TPU v7x, 32 devices: a whole 2x2x4 slice. The times are simulated.
32 devices in a mesh: px: 4 (over y, x), py: 8 (over z, core).
Axes of the slice: x: 2, y: 2, z: 4, core: 2. Of those that a mesh axis runs over, the one named last changes fastest.
Arguments:
- photons: float32 [1024, 128], P(('px', 'py')), may hold values from 50 to 1000
- halo_cells: int32 [1024, 128], P(('px', 'py')), may hold values from 0 to 1769471
- halo_counts: int32 [1024], P(('px', 'py')), may hold values from 1 to 128
- owners: int32 [1024, 1], P(('px', 'py')), may hold values from 0 to 7; in each aligned block of 32 rows (0 to 31, 32 to 63, ...) at most 4 rows name the same one
- density: float32 [384, 384, 384], P('px', 'py'), may hold values from 0.02 to 50
Outputs:
- fraction: float32 [384, 384, 384], P('px', 'py')
Inputs may be any that keep to these rules, and one draw needn't show every extreme that they name: The halos of a block all lie in pencil owners[b] of the block's own slab. Among the 32 blocks of one device no owner appears more than 4 times, a bound that some block reaches. Slots at or past halo_counts[b] are not live and carry arbitrary values. `halo_cells`: A cell index within the owner pencil is (x * 48 + y) * 384 + z with x, y, z local to that pencil.
All inputs are finite; a program needn't handle non-finite values.
Results may differ from a plain program's by a relative error of at most 0.0003.
Values sent between devices are 32-bit elements; how exact they have to be, the bound alone decides.
A program may use at most 192 MiB of HBM per device.

v0:
```python
import jax
import jax.numpy as jnp
import numpy as np
from jax import lax
from jax.sharding import PartitionSpec as P

CAP = 4
RADIUS = 20


def product(form, left, right):
    return jnp.einsum(form, left, right, precision=lax.Precision.HIGH)


def hartley(length):
    index_row = np.arange(length)
    angle = (index_row[:, None] * index_row[None, :] % length) * (2.0 * np.pi / length)
    return ((np.cos(angle) + np.sin(angle)) / np.sqrt(length)).astype(np.float32)


def top_hat(freq_x, freq_y, freq_z, grid):
    radial = jnp.sqrt(freq_x * freq_x + freq_y * freq_y + freq_z * freq_z) * (
        2.0 * jnp.pi * RADIUS / grid
    )
    safe = jnp.where(radial > 0, radial, 1.0)
    value = 3.0 * (jnp.sin(safe) - safe * jnp.cos(safe)) / (safe * safe * safe)
    return jnp.where(radial > 0, value, 1.0)


def on_device(photons, halo_cells, halo_counts, owners, density):
    rows_x, rows_y, grid = density.shape
    slots = photons.shape[1]
    count_x = lax.axis_size("px")
    count_y = lax.axis_size("py")
    place_y = lax.axis_index("py")
    devices_all = count_x * count_y
    planes = grid // devices_all
    area = rows_x * rows_y
    table = jnp.asarray(hartley(grid))
    table_x = table.reshape(count_x, rows_x, grid)
    table_y = table.reshape(count_y, rows_y, grid)

    def signed(index_values):
        return jnp.where(index_values < grid // 2, index_values, index_values - grid).astype(
            jnp.float32
        )

    freq = signed(jnp.arange(grid, dtype=jnp.int32))
    freq_z = signed(
        lax.axis_index(("px", "py")) * planes + jnp.arange(planes, dtype=jnp.int32)
    )
    window = top_hat(freq_z[:, None, None], freq[None, :, None], freq[None, None, :], grid)

    def smooth(field_rows):
        spec = product("az,zk->ka", field_rows, table)
        got = lax.all_to_all(
            spec.reshape(devices_all, planes, area),
            ("px", "py"), split_axis=0, concat_axis=0, tiled=True,
        )
        got = got.reshape(count_x, count_y, planes, rows_y, rows_x)
        half = product("iqklx,ixn->qkln", got, table_x)
        full = product("qkln,qlm->kmn", half, table_y) * window
        half = product("kmn,qlm->qkln", full, table_y)
        back = product("qkln,ixn->iqklx", half, table_x)
        got = lax.all_to_all(
            back.reshape(devices_all, planes, area),
            ("px", "py"), split_axis=0, concat_axis=0, tiled=True,
        )
        return product("ka,kz->az", got.reshape(grid, area), table)

    density_rows = density.transpose(1, 0, 2).reshape(area, grid)
    density_smooth = smooth(density_rows)

    slot_index = jnp.arange(slots, dtype=jnp.int32)[None, :]
    weights = jnp.where(slot_index < halo_counts[:, None], photons, 0.0)
    all_weights = lax.all_gather(weights, "py", axis=0, tiled=True)
    all_cells = lax.all_gather(halo_cells, "py", axis=0, tiled=True)
    all_owners = lax.all_gather(owners, "py", axis=0, tiled=True)[:, 0]
    owned = all_owners == place_y
    chosen = jnp.argsort(jnp.where(owned, 0, 1), stable=True)[: CAP * count_y]
    own_weights = jnp.where(owned[chosen][:, None], all_weights[chosen], 0.0)
    own_cells = all_cells[chosen]
    row = own_cells // grid
    spot = ((row % rows_y) * rows_x + row // rows_y) * grid + own_cells % grid
    painted = jnp.zeros((area * grid,), jnp.float32)
    painted = painted.at[spot.reshape(-1)].add(own_weights.reshape(-1))
    photon_smooth = smooth(painted.reshape(area, grid))

    fraction = jnp.clip(photon_smooth / jnp.maximum(density_smooth, 0.5), 0.0, 1.0)
    return fraction.reshape(rows_y, rows_x, grid).transpose(1, 0, 2)


def solution(mesh):
    placed = (
        P(("px", "py"), None),
        P(("px", "py"), None),
        P(("px", "py")),
        P(("px", "py"), None),
        P("px", "py", None),
    )
    return jax.shard_map(
        on_device, mesh=mesh, in_specs=placed, out_specs=P("px", "py", None), check_vma=False
    )
```

profile of v0, /device:TPU:0, one launch (start us, length us, event | category | flops | bytes accessed | tf_op | source)
XLA Modules:
  0.0 981.9 jit_solution(13321077338012238784)
XLA Ops:
  28.4 204.8 %all-reduce = s32[256]{0:T(256)S(1)} all-reduce(s32[256]{0:T(256)S(1)} %bitcast_dynamic-update-slice_fusion), channel_id=1, replica_groups=mesh['px'=4,'py'=8] {'py'}, use_global_device_ids=true, to_apply=%add | all-reduce | flops 256 | bytes 2048
  237.1 13.9 %all_gather.11 = f32[256,128]{1,0:T(8,128)S(1)} all-gather(f32[32,128]{1,0:T(8,128)S(1)} %fusion.35), channel_id=1, replica_groups=mesh['px'=4,'py'=8] {'py'}, dimensions={0}, use_global_device_ids=true | all-gather | bytes 147456 | tf_op jit(solution)/shard_map/all_gather | solution.py:76
  251.7 14.0 %all_gather.9 = s32[256,128]{1,0:T(8,128)S(1)} all-gather(s32[32,128]{1,0:T(8,128)S(1)} %copy-done.3), channel_id=1, replica_groups=mesh['px'=4,'py'=8] {'py'}, dimensions={0}, use_global_device_ids=true | all-gather | bytes 147456 | tf_op jit(solution)/shard_map/all_gather | solution.py:77
  266.5 25.3 %scatter_custom_fusion = f32[1769472]{0:T(1024)} fusion(s32[4096]{0:T(1024)S(1)} %bitcast.122, f32[4096]{0:T(1024)S(1)} %select_bitcast_fusion, f32[]{:T(128)} %constant.26.clone.1), kind=kCustom, calls=%fused_computation.29 | custom fusion | flops 4096 | bytes 7077892 | tf_op jit(solution)/shard_map/scatter-add | solution.py:86
  291.8 8.9 reshape.232
  300.7 12.5 %fusion.48 = f32[384,4608]{1,0:T(8,128)} fusion(f32[384,384]{1,0:T(8,128)S(1)} %copy-done.1, f32[4608,384]{1,0:T(8,128)} %reshape.232), kind=kOutput, calls=%fused_computation.73 | convolution fusion | flops 4076863488 | bytes 14745600 | tf_op jit(solution)/shard_map/az,zk->ka/dot_general | solution.py:12
  313.2 8.0 reshape.233
  325.4 11.2 %reshape.300 = f32[4,8,12,48,96]{4,3,2,1,0:T(8,128)} reshape(f32[32,12,4608]{2,1,0:T(8,128)} %all-to-all-done.2) | data formatting | bytes 14155776 | tf_op jit(solution)/shard_map/reshape | solution.py:60
  336.6 11.5 %fusion.26 = f32[8,12,48,384,1]{3,2,1,0,4:T(8,128)S(1)} fusion(f32[4,8,12,48,96]{4,3,2,1,0:T(8,128)} %reshape.300, f32[4,96,384,1,1]{2,1,0,4,3:T(8,128)S(1)} %copy-done), kind=kOutput, calls=%fused_computation.33 | convolution fusion | flops 4076863488 | bytes 14745600 | tf_op jit(solution)/shard_map/iqklx,ixn->qkln/dot_general | solution.py:12
  355.8 34.7 %fusion.11 = f32[12,384,8,48]{1,3,0,2:T(8,128)S(1)} fusion(f32[8,48,384,1]{2,1,3,0:T(8,128)S(1)} %copy-done.7, f32[12,384,384,1]{2,1,0,3:T(8,128)S(1)} %fusion.4, f32[384]{0:T(512)S(1)} %fusion.37, f32[12,384]{1,0:T(8,128)S(1)} %broadcast_add_fusion), kind=kOutput, calls=%fused_computation.21 | convolution fusion | flops 4098097152 | bytes 14765568 | tf_op jit(solution)/shard_map/kmn,qlm->qkln/dot_general | solution.py:12
  390.5 8.0 fusion.23
  403.5 11.7 %reshape.301 = f32[32,12,4608]{2,1,0:T(8,128)} reshape(f32[4,8,12,48,96]{4,3,2,1,0:T(8,128)} %copy.54) | data formatting | bytes 14155776 | tf_op jit(solution)/shard_map/reshape | solution.py:66
  415.1 117.4 %all-to-all-done = f32[32,12,4608]{2,1,0:T(8,128)} async-done(((f32[32,12,4608]{2,1,0:T(8,128)}), f32[32,12,4608]{2,1,0:T(8,128)}, u32[]{:S(2)}, u32[]{:S(2)}) %all-to-all-start) | async-done | bytes 7077920 | tf_op jit(solution)/shard_map/all_to_all | solution.py:56
  536.4 11.1 %reshape.298 = f32[4,8,12,48,96]{4,3,2,1,0:T(8,128)} reshape(f32[32,12,4608]{2,1,0:T(8,128)} %all-to-all-done) | data formatting | bytes 14155776 | tf_op jit(solution)/shard_map/reshape | solution.py:60
  547.6 11.4 %fusion.28 = f32[8,12,48,384,1]{3,2,1,0,4:T(8,128)S(1)} fusion(f32[4,8,12,48,96]{4,3,2,1,0:T(8,128)} %reshape.298, f32[4,96,384,1,1]{2,1,0,4,3:T(8,128)S(1)} %copy-done), kind=kOutput, calls=%fused_computation.35 | convolution fusion | flops 4076863488 | bytes 14745600 | tf_op jit(solution)/shard_map/iqklx,ixn->qkln/dot_general | solution.py:12
  566.6 34.7 %fusion.16 = f32[12,384,8,48]{1,3,0,2:T(8,128)S(1)} fusion(f32[8,48,384,1]{2,1,3,0:T(8,128)S(1)} %copy-done.7, f32[12,384,384,1]{2,1,0,3:T(8,128)S(1)} %fusion.6, f32[384]{0:T(512)S(1)} %fusion.37, f32[12,384]{1,0:T(8,128)S(1)} %broadcast_add_fusion), kind=kOutput, calls=%fused_computation.26 | convolution fusion | flops 4098097152 | bytes 14765568 | tf_op jit(solution)/shard_map/kmn,qlm->qkln/dot_general | solution.py:12
  601.4 8.0 fusion.20
  614.4 11.7 %reshape.299 = f32[32,12,4608]{2,1,0:T(8,128)} reshape(f32[4,8,12,48,96]{4,3,2,1,0:T(8,128)} %copy.50) | data formatting | bytes 14155776 | tf_op jit(solution)/shard_map/reshape | solution.py:66
  626.0 117.6 %all-to-all-done.3 = f32[32,12,4608]{2,1,0:T(8,128)} async-done(((f32[32,12,4608]{2,1,0:T(8,128)}), f32[32,12,4608]{2,1,0:T(8,128)}, u32[]{:S(2)}, u32[]{:S(2)}) %all-to-all-start.3) | async-done | bytes 7077920 | tf_op jit(solution)/shard_map/all_to_all | solution.py:65
  747.6 8.2 reshape.242
  755.8 11.0 %convolution_maximum_fusion = f32[4608,384]{1,0:T(8,128)} fusion(f32[384,4608]{1,0:T(8,128)} %reshape.242, f32[384,384]{1,0:T(8,128)S(1)} %copy-done.1), kind=kOutput, calls=%fused_computation.8 | convolution fusion | flops 4078632960 | bytes 14745600 | tf_op jit(solution)/shard_map/ka,kz->az/dot_general | solution.py:12
  766.8 188.0 %all-to-all-done.1 = f32[32,12,4608]{2,1,0:T(8,128)} async-done(((f32[32,12,4608]{2,1,0:T(8,128)}), f32[32,12,4608]{2,1,0:T(8,128)}, u32[]{:S(2)}, u32[]{:S(2)}) %all-to-all-start.1) | async-done | bytes 7077920 | tf_op jit(solution)/shard_map/all_to_all | solution.py:65
  954.8 8.2 reshape.238
  963.0 11.5 %divide_clamp_fusion = f32[4608,384]{1,0:T(8,128)S(1)} fusion(f32[4608,384]{1,0:T(8,128)} %convolution_maximum_fusion, f32[384,4608]{1,0:T(8,128)} %reshape.238, f32[384,384]{1,0:T(8,128)S(1)} %copy-done.1), kind=kOutput, calls=%fused_computation.28 | convolution fusion | flops 4080402432 | bytes 21823488 | tf_op jit(solution)/shard_map/ka,kz->az/dot_general | solution.py:12
  (50 shorter events, 77.3 us)
Async XLA Ops:
  0.0 5.4 copy-start.2
  19.5 7.5 copy-start.8
  19.5 8.7 copy-start.6
  19.5 217.5 %copy-start.4 = (f32[32,128]{1,0:T(8,128)S(1)}, f32[32,128]{1,0:T(8,128)}, u32[]{:S(2)}) copy-start(f32[32,128]{1,0:T(8,128)} %param.6) | copy-start | bytes 49156
  19.5 217.5 %copy-start.5 = (s32[32]{0:T(128)S(1)}, s32[32]{0:T(128)}, u32[]{:S(2)}) copy-start(s32[32]{0:T(128)} %param.8) | copy-start | bytes 388
  19.5 232.1 %copy-start.3 = (s32[32,128]{1,0:T(8,128)S(1)}, s32[32,128]{1,0:T(8,128)}, u32[]{:S(2)}) copy-start(s32[32,128]{1,0:T(8,128)} %param.7) | copy-start | bytes 49156
  19.5 301.7 %all-to-all-start.2 = ((f32[32,12,4608]{2,1,0:T(8,128)}), f32[32,12,4608]{2,1,0:T(8,128)}, u32[]{:S(2)}, u32[]{:S(2)}) async-start(f32[32,12,4608]{2,1,0:T(8,128)} %copy.32), calls=%async_computation.2 | async-start | bytes 18874368 | tf_op jit(solution)/shard_map/all_to_all | solution.py:56
  291.8 8.9 copy-start.1
  321.2 211.4 %all-to-all-start = ((f32[32,12,4608]{2,1,0:T(8,128)}), f32[32,12,4608]{2,1,0:T(8,128)}, u32[]{:S(2)}, u32[]{:S(2)}) async-start(f32[32,12,4608]{2,1,0:T(8,128)} %reshape.233), calls=%async_computation | async-start | bytes 18874368 | tf_op jit(solution)/shard_map/all_to_all | solution.py:56
  325.4 11.2 %copy-start = (f32[4,96,384,1,1]{2,1,0,4,3:T(8,128)S(1)}, f32[4,96,384,1,1]{2,1,0,4,3:T(8,128)}, u32[]{:S(2)}) copy-start(f32[4,96,384,1,1]{2,1,0,4,3:T(8,128)} %constant.88) | copy-start | bytes 1769476
  336.6 11.5 %copy-start.7 = (f32[8,48,384,1]{2,1,3,0:T(8,128)S(1)}, f32[8,48,384,1]{2,1,3,0:T(8,128)}, u32[]{:S(2)}) copy-start(f32[8,48,384,1]{2,1,3,0:T(8,128)} %constant.89) | copy-start | bytes 1769476
  532.6 211.1 %all-to-all-start.3 = ((f32[32,12,4608]{2,1,0:T(8,128)}), f32[32,12,4608]{2,1,0:T(8,128)}, u32[]{:S(2)}, u32[]{:S(2)}) async-start(f32[32,12,4608]{2,1,0:T(8,128)} %reshape.301), calls=%async_computation.3 | async-start | bytes 18874368 | tf_op jit(solution)/shard_map/all_to_all | solution.py:65
  743.7 211.2 %all-to-all-start.1 = ((f32[32,12,4608]{2,1,0:T(8,128)}), f32[32,12,4608]{2,1,0:T(8,128)}, u32[]{:S(2)}, u32[]{:S(2)}) async-start(f32[32,12,4608]{2,1,0:T(8,128)} %reshape.299), calls=%async_computation.1 | async-start | bytes 18874368 | tf_op jit(solution)/shard_map/all_to_all | solution.py:65
where the time goes:
time: 992 us; the launch traced here: 982 us
  waiting for transfers between devices  423 us (43%)
  blocking collectives  233 us (23%)
  matrix products  165 us (17%)
  local copies, waits for them, and re-layouts  112 us (11%)
  other arithmetic  28.9 us (3%)
  starting transfers between devices  19.3 us (2%)
    all_to_all x2, waiting for transfers between devices, smooth(): lax.all_to_all(back.reshape(devices_all, planes, area), ('px', 'py'), spl...  306 us
    unnamed x1, blocking collectives  205 us
    dot_general x12, matrix products, product(): return jnp.einsum(form, left, right, precision=lax.Precision.HIGH)  165 us
    all_to_all x2, waiting for transfers between devices, smooth(): lax.all_to_all(spec.reshape(devices_all, planes, area), ('px', 'py'), spl...  117 us
    reshape x4, local copies, waits for them, and re-layouts, smooth(): back.reshape(devices_all, planes, area)  33.2 us
    scatter-add x1, other arithmetic, on_device(): painted = painted.at[spot.reshape(-1)].add(own_weights.reshape(-1))  25.3 us
    reshape x2, local copies, waits for them, and re-layouts, smooth(): got = got.reshape(count_x, count_y, planes, rows_y, rows_x)  22.3 us
  transfers between devices with their start and end apart: 4, of which 3 were waited for; matrix products, arithmetic and copies ran while one was open for 26% of the time, Pallas kernels for 0%

commit v1 on v0

v1 whole, which is shorter than its diff:
```python
import jax
import jax.numpy as jnp
import numpy as np
from jax import lax
from jax.sharding import PartitionSpec as P

CAP = 4
RADIUS = 20
LANES = 128


def product(form, left, right):
    return jnp.einsum(form, left, right, precision=lax.Precision.HIGH)


def hartley(length):
    index_row = np.arange(length)
    angle = (index_row[:, None] * index_row[None, :] % length) * (2.0 * np.pi / length)
    return ((np.cos(angle) + np.sin(angle)) / np.sqrt(length)).astype(np.float32)


def top_hat(freq_x, freq_y, freq_z, grid):
    radial = jnp.sqrt(freq_x * freq_x + freq_y * freq_y + freq_z * freq_z) * (
        2.0 * jnp.pi * RADIUS / grid
    )
    safe = jnp.where(radial > 0, radial, 1.0)
    value = 3.0 * (jnp.sin(safe) - safe * jnp.cos(safe)) / (safe * safe * safe)
    return jnp.where(radial > 0, value, 1.0)


def on_device(photons, halo_cells, halo_counts, owners, density):
    rows_x, rows_y, grid = density.shape
    blocks, slots = photons.shape
    count_x = lax.axis_size("px")
    count_y = lax.axis_size("py")
    place_y = lax.axis_index("py")
    devices_all = count_x * count_y
    planes = grid // devices_all
    area = rows_x * rows_y
    table = jnp.asarray(hartley(grid))
    table_x = table.reshape(count_x, rows_x, grid)
    table_y = table.reshape(count_y, rows_y, grid)

    assert area * grid < 1 << 24
    slot_index = jnp.arange(slots, dtype=jnp.int32)[None, :]
    weights = jnp.where(slot_index < halo_counts[:, None], photons, 0.0)
    row = halo_cells // grid
    spot = ((row % rows_y) * rows_x + row // rows_y) * grid + halo_cells % grid
    owner_row = jnp.broadcast_to(owners, (blocks, slots))
    sent = jnp.stack([weights, spot.astype(jnp.float32), owner_row.astype(jnp.float32)])
    slab = lax.all_gather(sent, "py", axis=1, tiled=True)
    slab, density = lax.optimization_barrier((slab, density))

    def signed(index_values):
        return jnp.where(index_values < grid // 2, index_values, index_values - grid).astype(
            jnp.float32
        )

    def exchange(blocks_out):
        got = lax.all_to_all(
            blocks_out.reshape(devices_all, planes * area // LANES, LANES),
            ("px", "py"), split_axis=0, concat_axis=0, tiled=True,
        )
        return got

    def forward(field_rows):
        spec = product("az,zk->ka", field_rows, table)
        return exchange(spec)

    def middle(got):
        got = got.reshape(count_x, count_y, planes, rows_y, rows_x)
        half = product("iqklx,ixn->qkln", got, table_x)
        full = product("qkln,qlm->kmn", half, table_y) * window
        half = product("kmn,qlm->qkln", full, table_y)
        back = product("qkln,ixn->iqklx", half, table_x)
        return exchange(back)

    def backward(got):
        return product("ka,kz->az", got.reshape(grid, area), table)

    density_rows = density.transpose(1, 0, 2).reshape(area, grid)
    density_spec = forward(density_rows)

    freq = signed(jnp.arange(grid, dtype=jnp.int32))
    freq_z = signed(
        lax.axis_index(("px", "py")) * planes + jnp.arange(planes, dtype=jnp.int32)
    )
    window = top_hat(freq_z[:, None, None], freq[None, :, None], freq[None, None, :], grid)
    window = lax.optimization_barrier(window)

    owned = slab[2, :, 0] == place_y.astype(jnp.float32)
    chosen = jnp.argsort(jnp.where(owned, 0, 1), stable=True)[: CAP * count_y]
    own_weights = jnp.where(owned[chosen][:, None], slab[0][chosen], 0.0)
    own_spot = slab[1][chosen].astype(jnp.int32)
    painted = jnp.zeros((area * grid,), jnp.float32)
    painted = painted.at[own_spot.reshape(-1)].add(own_weights.reshape(-1))
    photon_spec = forward(painted.reshape(area, grid))

    density_smooth = backward(middle(density_spec))
    photon_smooth = backward(middle(photon_spec))

    fraction = jnp.clip(photon_smooth / jnp.maximum(density_smooth, 0.5), 0.0, 1.0)
    return fraction.reshape(rows_y, rows_x, grid).transpose(1, 0, 2)


def solution(mesh):
    placed = (
        P(("px", "py"), None),
        P(("px", "py"), None),
        P(("px", "py")),
        P(("px", "py"), None),
        P("px", "py", None),
    )
    return jax.shard_map(
        on_device, mesh=mesh, in_specs=placed, out_specs=P("px", "py", None), check_vma=False
    )
```

time: 992 us -> 722 us (0.73)
  blocking collectives: 233 us -> 16.2 us
  matrix products: 165 us -> 124 us
  waiting for transfers between devices: 423 us -> 390 us
  other arithmetic: 28.9 us -> 61.4 us
    unnamed x1 -> x0, blocking collectives: 205 us -> none
    dot_general x12, matrix products: 165 us -> 124 us  [product(): return jnp.einsum(form, left, right, precision=lax.Precision.HIGH)]
    all_to_all x4, waiting for transfers between devices: 423 us -> 390 us  [exchange(): lax.all_to_all(blocks_out.reshape(devices_all, planes * area // LANES, LA...]
    select_n x4, other arithmetic: 0.37 us -> 30.3 us  [the longest x1 30.2 us: top_hat(): return jnp.where(radial > 0, value, 1.0)]
    all_gather x2 -> x1, blocking collectives: 27.9 us -> 16.2 us  [on_device(): slab = lax.all_gather(sent, 'py', axis=1, tiled=True)]
    reshape x10 -> x9, local copies, waits for them, and re-layouts: 88.7 us -> 80 us  [the longest x4 36.7 us: exchange(): blocks_out.reshape(devices_all, planes * area // LANES, LANES)]
  transfers between devices with their start and end apart: 4 -> 4, of which waited for: 3 -> 4; matrix products, arithmetic and copies ran while one was open for 26% -> 33% of each run, Pallas kernels for 0% -> 0%
where the time goes in v1:
time: 722 us; the launch traced here: 713 us
  waiting for transfers between devices  390 us (54%)
  matrix products  124 us (17%)
  local copies, waits for them, and re-layouts  104 us (14%)
  other arithmetic  61.4 us (9%)
  starting transfers between devices  16.9 us (2%)
  blocking collectives  16.2 us (2%)
    all_to_all x4, waiting for transfers between devices, exchange(): lax.all_to_all(blocks_out.reshape(devices_all, planes * area // LANES, LA...  390 us
    dot_general x12, matrix products, product(): return jnp.einsum(form, left, right, precision=lax.Precision.HIGH)  124 us
    reshape x4, local copies, waits for them, and re-layouts, exchange(): blocks_out.reshape(devices_all, planes * area // LANES, LANES)  36.7 us
    select_n x1, other arithmetic, top_hat(): return jnp.where(radial > 0, value, 1.0)  30.2 us
    scatter-add x1, other arithmetic, on_device(): painted = painted.at[own_spot.reshape(-1)].add(own_weights.reshape(-1))  25.5 us
    reshape x2, local copies, waits for them, and re-layouts, middle(): got = got.reshape(count_x, count_y, planes, rows_y, rows_x)  19.3 us
    all_to_all x4, starting transfers between devices, exchange(): lax.all_to_all(blocks_out.reshape(devices_all, planes * area // LANES, LA...  16.9 us
    all_gather x1, blocking collectives, on_device(): slab = lax.all_gather(sent, 'py', axis=1, tiled=True)  16.2 us
  transfers between devices with their start and end apart: 4, of which 4 were waited for; matrix products, arithmetic and copies ran while one was open for 33% of the time, Pallas kernels for 0%

profile of v1, /device:TPU:0, one launch (start us, length us, event | category | flops | bytes accessed | tf_op | source)
XLA Modules:
  0.0 712.7 jit_solution(3844486855548637540)
XLA Ops:
  2.3 16.2 %all_gather.3 = f32[3,256,128]{2,1,0:T(8,128)S(1)} all-gather(f32[3,32,128]{2,1,0:T(8,128)S(1)} %pad_maximum_fusion), channel_id=1, replica_groups=mesh['px'=4,'py'=8] {'py'}, dimensions={1}, use_global_device_ids=true | all-gather | bytes 442368 | tf_op jit(solution)/shard_map/all_gather | solution.py:51
  23.9 11.0 %fusion.46 = f32[384,4608]{1,0:T(8,128)} fusion(f32[384,384]{1,0:T(8,128)S(1)} %copy-done, f32[4608,384]{1,0:T(8,128)S(1)} %bitcast.97), kind=kOutput, calls=%fused_computation.75 | convolution fusion | flops 4076863488 | bytes 14745600 | tf_op jit(solution)/shard_map/az,zk->ka/dot_general | solution.py:13
  53.3 25.5 %scatter_custom_fusion = f32[1769472]{0:T(1024)} fusion(s32[4096]{0:T(1024)S(1)} %bitcast.104, f32[4096]{0:T(1024)S(1)} %select_bitcast_fusion, f32[]{:T(128)} %constant.26.clone.1), kind=kCustom, calls=%fused_computation.35 | custom fusion | flops 4096 | bytes 7077892 | tf_op jit(solution)/shard_map/scatter-add | solution.py:96
  78.8 8.8 %reshape.135 = f32[4608,384]{1,0:T(8,128)} reshape(f32[1769472]{0:T(1024)} %scatter_custom_fusion) | data formatting | bytes 14155776 | tf_op jit(solution)/shard_map/reshape | solution.py:97
  87.6 13.0 %fusion.45 = f32[384,4608]{1,0:T(8,128)} fusion(f32[384,384]{1,0:T(8,128)S(1)} %copy-done, f32[4608,384]{1,0:T(8,128)} %reshape.135), kind=kOutput, calls=%fused_computation.74 | convolution fusion | flops 4076863488 | bytes 14745600 | tf_op jit(solution)/shard_map/az,zk->ka/dot_general | solution.py:13
  108.0 96.7 %all-to-all-done.2 = f32[32,432,128]{2,1,0:T(8,128)} async-done(((f32[32,432,128]{2,1,0:T(8,128)}), f32[32,432,128]{2,1,0:T(8,128)}, u32[]{:S(2)}, u32[]{:S(2)}) %all-to-all-start.2) | async-done | bytes 7077920 | tf_op jit(solution)/shard_map/all_to_all | solution.py:60
  208.5 30.2 %compare_select_fusion = f32[12,384,384]{1,2,0:T(8,128)} fusion(f32[384]{0:T(512)S(1)} %fusion.42, f32[12,384]{1,0:T(8,128)S(1)} %broadcast_add_fusion), kind=kLoop, calls=%fused_computation.10 | loop fusion | flops 19464192 | bytes 7097856 | tf_op jit(solution)/shard_map/jit(_where)/select_n | solution.py:28
  238.7 9.7 %reshape.144 = f32[4,8,12,48,96]{4,3,2,1,0:T(8,128)} reshape(f32[32,432,128]{2,1,0:T(8,128)} %all-to-all-done.2) | data formatting | bytes 14155776 | tf_op jit(solution)/shard_map/reshape | solution.py:71
  248.4 20.4 %fusion = f32[8,12,48,384,1]{3,2,0,1,4:T(8,128)S(1)} fusion(f32[4,96,384,1,1]{2,1,3,4,0:T(8,128)S(1)} %copy-done.2, f32[4,8,12,48,96]{4,3,2,1,0:T(8,128)} %reshape.144), kind=kOutput, calls=%fused_computation.6 | convolution fusion | flops 4076863488 | bytes 14745600 | tf_op jit(solution)/shard_map/iqklx,ixn->qkln/dot_general | solution.py:13
  268.7 8.0 %fusion.18 = f32[12,384,384,1]{2,1,0,3:T(8,128)S(1)} fusion(f32[8,48,384,1]{2,1,3,0:T(8,128)S(1)} %copy-done.1, f32[8,12,48,384,1]{3,2,0,1,4:T(8,128)S(1)} %fusion), kind=kOutput, calls=%fused_computation.27 | convolution fusion | flops 4076863488 | bytes 14745600 | tf_op jit(solution)/shard_map/qkln,qlm->kmn/dot_general | solution.py:13
  283.3 8.0 %fusion.29 = f32[4,8,12,48,96]{4,3,0,2,1:T(8,128)S(1)} fusion(f32[4,96,384,1,1]{2,1,0,4,3:T(8,128)S(1)} %copy-done.3, f32[12,384,8,48]{1,3,0,2:T(8,128)S(1)} %fusion.11), kind=kOutput, calls=%fused_computation.38 | convolution fusion | flops 4076863488 | bytes 14745600 | tf_op jit(solution)/shard_map/qkln,ixn->iqklx/dot_general | solution.py:13
  296.2 11.0 %reshape.145 = f32[32,432,128]{2,1,0:T(8,128)} reshape(f32[4,8,12,48,96]{4,3,2,1,0:T(8,128)} %copy.10) | data formatting | bytes 14155776 | tf_op jit(solution)/shard_map/reshape | solution.py:61
  307.2 57.9 %all-to-all-done = f32[32,432,128]{2,1,0:T(8,128)} async-done(((f32[32,432,128]{2,1,0:T(8,128)}), f32[32,432,128]{2,1,0:T(8,128)}, u32[]{:S(2)}, u32[]{:S(2)}) %all-to-all-start) | async-done | bytes 7077920 | tf_op jit(solution)/shard_map/all_to_all | solution.py:60
  368.7 9.6 %reshape.137 = f32[4,8,12,48,96]{4,3,2,1,0:T(8,128)} reshape(f32[32,432,128]{2,1,0:T(8,128)} %all-to-all-done) | data formatting | bytes 14155776 | tf_op jit(solution)/shard_map/reshape | solution.py:71
  378.3 11.8 %fusion.2 = f32[8,12,48,384,1]{3,2,0,1,4:T(8,128)S(1)} fusion(f32[4,96,384,1,1]{2,1,3,4,0:T(8,128)S(1)} %copy-done.2, f32[4,8,12,48,96]{4,3,2,1,0:T(8,128)} %reshape.137), kind=kOutput, calls=%fused_computation.8 | convolution fusion | flops 4076863488 | bytes 14745600 | tf_op jit(solution)/shard_map/iqklx,ixn->qkln/dot_general | solution.py:13
  390.1 8.0 %fusion.20 = f32[12,384,384,1]{2,1,0,3:T(8,128)S(1)} fusion(f32[8,48,384,1]{2,1,3,0:T(8,128)S(1)} %copy-done.1, f32[8,12,48,384,1]{3,2,0,1,4:T(8,128)S(1)} %fusion.2), kind=kOutput, calls=%fused_computation.29 | convolution fusion | flops 4076863488 | bytes 14745600 | tf_op jit(solution)/shard_map/qkln,qlm->kmn/dot_general | solution.py:13
  404.4 8.0 %fusion.26 = f32[4,8,12,48,96]{4,3,0,2,1:T(8,128)S(1)} fusion(f32[4,96,384,1,1]{2,1,0,4,3:T(8,128)S(1)} %copy-done.3, f32[12,384,8,48]{1,3,0,2:T(8,128)S(1)} %fusion.16), kind=kOutput, calls=%fused_computation.37 | convolution fusion | flops 4076863488 | bytes 14745600 | tf_op jit(solution)/shard_map/qkln,ixn->iqklx/dot_general | solution.py:13
  417.4 11.0 %reshape.140 = f32[32,432,128]{2,1,0:T(8,128)} reshape(f32[4,8,12,48,96]{4,3,2,1,0:T(8,128)} %copy.8) | data formatting | bytes 14155776 | tf_op jit(solution)/shard_map/reshape | solution.py:61
  428.3 97.1 %all-to-all-done.3 = f32[32,432,128]{2,1,0:T(8,128)} async-done(((f32[32,432,128]{2,1,0:T(8,128)}), f32[32,432,128]{2,1,0:T(8,128)}, u32[]{:S(2)}, u32[]{:S(2)}) %all-to-all-start.3) | async-done | bytes 7077920 | tf_op jit(solution)/shard_map/all_to_all | solution.py:60
  529.3 7.6 %reshape.146 = f32[384,4608]{1,0:T(8,128)} reshape(f32[32,432,128]{2,1,0:T(8,128)} %all-to-all-done.3) | data formatting | bytes 14155776 | tf_op jit(solution)/shard_map/reshape | solution.py:79
  536.9 11.0 %convolution_maximum_fusion = f32[4608,384]{1,0:T(8,128)} fusion(f32[384,4608]{1,0:T(8,128)} %reshape.146, f32[384,384]{1,0:T(8,128)S(1)} %copy-done), kind=kOutput, calls=%fused_computation.12 | convolution fusion | flops 4078632960 | bytes 14745600 | tf_op jit(solution)/shard_map/ka,kz->az/dot_general | solution.py:13
  548.0 138.0 %all-to-all-done.1 = f32[32,432,128]{2,1,0:T(8,128)} async-done(((f32[32,432,128]{2,1,0:T(8,128)}), f32[32,432,128]{2,1,0:T(8,128)}, u32[]{:S(2)}, u32[]{:S(2)}) %all-to-all-start.1) | async-done | bytes 7077920 | tf_op jit(solution)/shard_map/all_to_all | solution.py:60
  686.0 7.6 %reshape.141 = f32[384,4608]{1,0:T(8,128)} reshape(f32[32,432,128]{2,1,0:T(8,128)} %all-to-all-done.1) | data formatting | bytes 14155776 | tf_op jit(solution)/shard_map/reshape | solution.py:79
  693.6 11.6 %divide_clamp_fusion = f32[4608,384]{1,0:T(8,128)S(1)} fusion(f32[4608,384]{1,0:T(8,128)} %convolution_maximum_fusion, f32[384,4608]{1,0:T(8,128)} %reshape.141, f32[384,384]{1,0:T(8,128)S(1)} %copy-done), kind=kOutput, calls=%fused_computation.34 | convolution fusion | flops 4080402432 | bytes 21823488 | tf_op jit(solution)/shard_map/ka,kz->az/dot_general | solution.py:13
  (51 shorter events, 74.2 us)
Async XLA Ops:
  18.5 5.4 copy-start
  42.2 162.5 %all-to-all-start.2 = ((f32[32,432,128]{2,1,0:T(8,128)}), f32[32,432,128]{2,1,0:T(8,128)}, u32[]{:S(2)}, u32[]{:S(2)}) async-start(f32[32,432,128]{2,1,0:T(8,128)} %reshape.143), calls=%async_computation.2 | async-start | bytes 14155776 | tf_op jit(solution)/shard_map/all_to_all | solution.py:60
  204.7 160.3 %all-to-all-start = ((f32[32,432,128]{2,1,0:T(8,128)}), f32[32,432,128]{2,1,0:T(8,128)}, u32[]{:S(2)}, u32[]{:S(2)}) async-start(f32[32,432,128]{2,1,0:T(8,128)} %reshape.136), calls=%async_computation | async-start | bytes 14155776 | tf_op jit(solution)/shard_map/all_to_all | solution.py:60
  238.7 9.7 %copy-start.2 = (f32[4,96,384,1,1]{2,1,3,4,0:T(8,128)S(1)}, f32[4,96,384,1,1]{2,1,3,4,0:T(8,128)}, u32[]{:S(2)}) copy-start(f32[4,96,384,1,1]{2,1,3,4,0:T(8,128)} %constant.80) | copy-start | bytes 1769476
  248.3 20.4 %copy-start.1 = (f32[8,48,384,1]{2,1,3,0:T(8,128)S(1)}, f32[8,48,384,1]{2,1,3,0:T(8,128)}, u32[]{:S(2)}) copy-start(f32[8,48,384,1]{2,1,3,0:T(8,128)} %constant.81) | copy-start | bytes 1769476
  248.4 28.4 %slice-start = ((s8[7077888]{0:T(1024)(128)(4,1)}), s8[4194304]{0:T(1024)(128)(4,1)S(1)}, s32[]{:S(2)}) async-start(s8[7077888]{0:T(1024)(128)(4,1)} %bitcast.98), calls=%async_computation.4 | async-start | bytes 8388608
  268.7 8.0 %slice-start.1 = ((s8[7077888]{0:T(1024)(128)(4,1)}), s8[2883584]{0:T(1024)(128)(4,1)S(1)}, s32[]{:S(2)}) async-start(s8[7077888]{0:T(1024)(128)(4,1)} %bitcast.98), calls=%async_computation.5 | async-start | bytes 5767168
  276.8 6.5 copy-start.3
  365.1 160.3 %all-to-all-start.3 = ((f32[32,432,128]{2,1,0:T(8,128)}), f32[32,432,128]{2,1,0:T(8,128)}, u32[]{:S(2)}, u32[]{:S(2)}) async-start(f32[32,432,128]{2,1,0:T(8,128)} %reshape.145), calls=%async_computation.3 | async-start | bytes 14155776 | tf_op jit(solution)/shard_map/all_to_all | solution.py:60
  378.3 19.8 %slice-start.2 = ((s8[7077888]{0:T(1024)(128)(4,1)}), s8[4194304]{0:T(1024)(128)(4,1)S(1)}, s32[]{:S(2)}) async-start(s8[7077888]{0:T(1024)(128)(4,1)} %bitcast.100), calls=%async_computation.6 | async-start | bytes 8388608
  390.1 8.0 %slice-start.3 = ((s8[7077888]{0:T(1024)(128)(4,1)}), s8[2883584]{0:T(1024)(128)(4,1)S(1)}, s32[]{:S(2)}) async-start(s8[7077888]{0:T(1024)(128)(4,1)} %bitcast.100), calls=%async_computation.7 | async-start | bytes 5767168
  525.4 160.6 %all-to-all-start.1 = ((f32[32,432,128]{2,1,0:T(8,128)}), f32[32,432,128]{2,1,0:T(8,128)}, u32[]{:S(2)}, u32[]{:S(2)}) async-start(f32[32,432,128]{2,1,0:T(8,128)} %reshape.140), calls=%async_computation.1 | async-start | bytes 14155776 | tf_op jit(solution)/shard_map/all_to_all | solution.py:60

commit v2 on v1

v2 whole, which is shorter than its diff:
```python
import jax
import jax.numpy as jnp
import numpy as np
from jax import lax
from jax.experimental import pallas as pl
from jax.experimental.pallas import tpu as pltpu
from jax.sharding import PartitionSpec as P

RADIUS = 20
LANES = 128
UNROLL = 8
TAB_BITS = 10


def product(form, left, right):
    return jnp.einsum(form, left, right, precision=lax.Precision.HIGH)


def hartley(length):
    index_row = np.arange(length)
    angle = (index_row[:, None] * index_row[None, :] % length) * (2.0 * np.pi / length)
    return ((np.cos(angle) + np.sin(angle)) / np.sqrt(length)).astype(np.float32)


def sine_cosine(angle):
    turns = jnp.round(angle * np.float32(2.0 / np.pi))
    rest = angle - turns * np.float32(1.5703125)
    rest = rest - turns * np.float32(4.837512969970703e-4)
    rest = rest - turns * np.float32(7.549789948768648e-8)
    square = rest * rest
    sine = ((-1.9515295891e-4 * square + 8.3321608736e-3) * square - 1.6666654611e-1) * (
        square * rest
    ) + rest
    cosine = (
        (2.443315711809948e-5 * square - 1.388731625493765e-3) * square + 4.166664568298827e-2
    ) * (square * square) + (1.0 - 0.5 * square)
    quarter = turns.astype(jnp.int32)
    swap = (quarter & 1) == 1
    first, second = jnp.where(swap, cosine, sine), jnp.where(swap, sine, cosine)
    first = jnp.where((quarter & 2) == 2, -first, first)
    second = jnp.where(((quarter + 1) & 2) == 2, -second, second)
    return first, second


def top_hat(freq_x, freq_y, freq_z, grid):
    radial = jnp.sqrt(freq_x * freq_x + freq_y * freq_y + freq_z * freq_z) * (
        2.0 * jnp.pi * RADIUS / grid
    )
    safe = jnp.where(radial > 0, radial, 1.0)
    sine, cosine = sine_cosine(safe)
    value = 3.0 * (sine - safe * cosine) / (safe * safe * safe)
    return jnp.where(radial > 0, value, 1.0)


def paint_kernel(key, weight, count, waves, out, other):
    rows = out.shape[0]
    step = 256
    sums = (out, other)

    @pl.loop(0, rows // step)
    def _(index):
        part = pl.ds(pl.multiple_of(index * step, step), step)
        for total in sums:
            total[part, :] = jnp.zeros((step, LANES), jnp.float32)

    @pl.loop(0, key.shape[0])
    def _(block):
        turns = lax.div(count[block] + (UNROLL - 1), UNROLL)

        @pl.loop(0, turns)
        def _(turn):
            for lane in range(UNROLL):
                slot = turn * UNROLL + lane
                both = key[block, slot]
                row = pl.ds(lax.shift_right_logical(both, TAB_BITS), 1)
                wave = pl.ds(lax.bitwise_and(both, (1 << TAB_BITS) - 1), 1)
                total = sums[lane % len(sums)]
                total[row, :] = total[row, :] + weight[block, slot] * waves[wave, :]

    @pl.loop(0, rows // step)
    def _(index):
        part = pl.ds(pl.multiple_of(index * step, step), step)
        out[part, :] = out[part, :] + other[part, :]


def paint(key, weight, count, waves, rows):
    smem = pl.BlockSpec(memory_space=pltpu.SMEM)
    vmem = pl.BlockSpec(memory_space=pltpu.VMEM)
    return pl.pallas_call(
        paint_kernel,
        out_shape=jax.ShapeDtypeStruct((rows, LANES), jnp.float32),
        in_specs=[smem, smem, smem, vmem],
        out_specs=vmem,
        scratch_shapes=[pltpu.VMEM((rows, LANES), jnp.float32)],
        cost_estimate=pl.CostEstimate(
            flops=80_000_000_000, bytes_accessed=rows * LANES * 4, transcendentals=0
        ),
        compiler_params=pltpu.CompilerParams(vmem_limit_bytes=3 * rows * LANES * 4),
        name="paint",
    )(key, weight, count, waves)


def on_device(photons, halo_cells, halo_counts, owners, density):
    rows_x, rows_y, grid = density.shape
    slots = photons.shape[1]
    count_x = lax.axis_size("px")
    count_y = lax.axis_size("py")
    place_x = lax.axis_index("px")
    place_y = lax.axis_index("py")
    devices_all = count_x * count_y
    planes = grid // devices_all
    area = rows_x * rows_y
    table_np = hartley(grid)
    table = jnp.asarray(table_np)
    table_x = table.reshape(count_x, rows_x, grid)
    table_y = table.reshape(count_y, rows_y, grid)

    first = max(1, planes * 2 // 3)
    parts = [(0, first)] + ([(first, planes)] if first < planes else [])
    by_plane = table_np.reshape(grid, devices_all, planes)
    tables = [
        jnp.asarray(np.ascontiguousarray(by_plane[:, :, a:b]).reshape(grid, devices_all * (b - a)))
        for a, b in parts
    ]

    pair = LANES // 2
    width = pair // count_x
    assert planes <= width and rows_x % 2 == 0
    assert 2 * grid <= 1 << TAB_BITS and rows_x * grid * grid < 1 << 24
    half_x = rows_x // 2
    rows = grid * half_x
    slot_index = jnp.arange(slots, dtype=jnp.int32)[None, :]
    live = slot_index < halo_counts[:, None]
    weights = jnp.where(live, photons, 0.0)
    cell_x = halo_cells // (rows_y * grid)
    cell_y = owners * rows_y + halo_cells // grid % rows_y
    cell_z = halo_cells % grid
    row = (cell_x // 2) * grid + cell_y
    key = jnp.where(live, row * (2 * grid) + (cell_x % 2) * grid + cell_z, 0)
    sent = jnp.stack([weights, key.astype(jnp.float32)])
    slab = lax.all_gather(sent, "py", axis=1, tiled=True)
    slab, density = lax.optimization_barrier((slab, density))

    def signed(index_values):
        return jnp.where(index_values < grid // 2, index_values, index_values - grid).astype(
            jnp.float32
        )

    received = []

    def exchange(blocks_out):
        blocks_out = blocks_out.reshape(devices_all, -1, LANES)
        if received:
            blocks_out, _ = lax.optimization_barrier((blocks_out, received[-1]))
        got = lax.all_to_all(
            blocks_out, ("px", "py"), split_axis=0, concat_axis=0, tiled=True
        )
        received.append(got)
        return got

    density_rows = density.transpose(1, 0, 2).reshape(area, grid)
    specs = [product("az,zk->ka", density_rows, part) for part in tables]
    density_got = [exchange(specs[0])]

    freq = signed(jnp.arange(grid, dtype=jnp.int32))
    freq_z = signed(
        lax.axis_index(("px", "py")) * planes + jnp.arange(planes, dtype=jnp.int32)
    )
    windows = [
        lax.optimization_barrier(
            top_hat(freq_z[a:b, None, None], freq[None, :, None], freq[None, None, :], grid)
        )
        for a, b in parts
    ]

    all_keys = slab[1].astype(jnp.int32)
    all_keys = all_keys // (2 * grid) * (1 << TAB_BITS) + all_keys % (2 * grid)
    all_counts = jnp.max(jnp.where(slab[0] != 0.0, slot_index + 1, 0), axis=1)
    own = lax.dynamic_index_in_dim(
        table.reshape(grid, count_x, count_y, planes), place_y, 2, keepdims=False
    )
    own = jnp.pad(own, ((0, 0), (0, 0), (0, width - planes))).reshape(grid, pair)
    waves = jnp.concatenate(
        [jnp.pad(own, ((0, 0), (0, pair))), jnp.pad(own, ((0, 0), (pair, 0)))]
    )
    painted = paint(all_keys, slab[0], all_counts, waves, rows)
    for spec in specs[1:]:
        spec, painted, windows[0] = lax.optimization_barrier((spec, painted, windows[0]))
        density_got.append(exchange(spec))

    def outward(full):
        half = product("kmn,qlm->qkln", full, table_y)
        back = product("qkln,ixn->iqklx", half, table_x)
        return exchange(back)

    def inward(got):
        got = got.reshape(count_x, count_y, -1, rows_y, rows_x)
        half = product("iqklx,ixn->qkln", got, table_x)
        return product("qkln,qlm->kmn", half, table_y)

    lines = product("ayc,ym->acm", painted.reshape(half_x, grid, LANES), table)
    lines = lines.reshape(rows_x, count_x, width, grid)[:, :, :planes]
    lines = lines.transpose(1, 2, 0, 3)
    rows_of = [
        lax.dynamic_index_in_dim(table_x, (place_x - shift) % count_x, 0, keepdims=False)
        for shift in range(count_x)
    ]
    photon_parts = [
        [
            lax.dynamic_slice(
                lines, ((place_x + shift) % count_x, a, 0, 0), (1, b - a, rows_x, grid)
            )[0]
            for shift in range(count_x)
        ]
        for a, b in parts
    ]

    def around(block, shift):
        if shift == 0:
            return block
        return lax.ppermute(block, "px", [(i, (i + shift) % count_x) for i in range(count_x)])

    photon_parts = [
        [around(block, shift) for shift, block in enumerate(blocks)]
        for blocks in photon_parts
    ]

    def crosswise(blocks):
        total = None
        for block, rows_from in zip(blocks, rows_of):
            term = product("kxm,xn->kmn", block, rows_from)
            total = term if total is None else total + term
        return total

    density_back = [outward(inward(got) * win) for got, win in zip(density_got, windows)]
    photon_back = [
        outward(crosswise(blocks) * win) for blocks, win in zip(photon_parts, windows)
    ]

    def backward(got):
        total = None
        for part, waves in zip(got, tables):
            term = product("ka,zk->az", part.reshape(-1, area), waves)
            total = term if total is None else total + term
        return total

    density_smooth = backward(density_back)
    photon_smooth = backward(photon_back)

    fraction = jnp.clip(photon_smooth / jnp.maximum(density_smooth, 0.5), 0.0, 1.0)
    return fraction.reshape(rows_y, rows_x, grid).transpose(1, 0, 2)


def solution(mesh):
    placed = (
        P(("px", "py"), None),
        P(("px", "py"), None),
        P(("px", "py")),
        P(("px", "py"), None),
        P("px", "py", None),
    )

    return jax.shard_map(
        on_device, mesh=mesh, in_specs=placed, out_specs=P("px", "py", None), check_vma=False
    )
```

time: 722 us -> 637 us (0.88)
  waiting for transfers between devices: 390 us -> 203 us
  Pallas kernels: 0 us -> 79.9 us
  other arithmetic: 61.4 us -> 17.5 us
  starting transfers between devices: 16.9 us -> 55.2 us
  matrix products: 124 us -> 151 us
    all_to_all x4 -> x6, waiting for transfers between devices: 390 us -> 94.6 us  [exchange(): lax.all_to_all(blocks_out, ('px', 'py'), split_axis=0, concat_axis=0, til...]
    ppermute x0 -> x6, waiting for transfers between devices: none -> 108 us  [around(): lax.ppermute(block, 'px', [(i, (i + shift) % count_x) for i in range(coun...]
    pallas_call x0 -> x1, Pallas kernels: none -> 79.9 us  [paint(): pl.pallas_call(paint_kernel, out_shape=jax.ShapeDtypeStruct((rows, LANES)...]
    all_to_all x4 -> x6, starting transfers between devices: 16.9 us -> 45.7 us  [exchange(): lax.all_to_all(blocks_out, ('px', 'py'), split_axis=0, concat_axis=0, til...]
    dot_general x12 -> x27, matrix products: 124 us -> 151 us  [product(): return jnp.einsum(form, left, right, precision=lax.Precision.HIGH)]
    scatter-add x1 -> x0, other arithmetic: 25.5 us -> none  [on_device(): painted = painted.at[own_spot.reshape(-1)].add(own_weights.reshape(-1))]
    reshape x9 -> x13, local copies, waits for them, and re-layouts: 80 us -> 57.3 us  [the longest x6 30 us: exchange(): blocks_out = blocks_out.reshape(devices_all, -1, LANES)]
    select_n x1 -> x2, other arithmetic: 30.2 us -> 14.8 us  [top_hat(): return jnp.where(radial > 0, value, 1.0)]
  transfers between devices with their start and end apart: 4 -> 12, of which waited for: 4 -> 8; matrix products, arithmetic and copies ran while one was open for 33% -> 36% of each run, Pallas kernels for 0% -> 13%
where the time goes in v2:
time: 637 us; the launch traced here: 627 us
  waiting for transfers between devices  203 us (32%)
  matrix products  151 us (24%)
  local copies, waits for them, and re-layouts  104 us (16%)
  Pallas kernels  79.9 us (13%)
  starting transfers between devices  55.2 us (9%)
  other arithmetic  17.5 us (3%)
  blocking collectives  15.9 us (2%)
    dot_general x27, matrix products, product(): return jnp.einsum(form, left, right, precision=lax.Precision.HIGH)  151 us
    ppermute x6, waiting for transfers between devices, around(): lax.ppermute(block, 'px', [(i, (i + shift) % count_x) for i in range(coun...  108 us
    all_to_all x6, waiting for transfers between devices, exchange(): lax.all_to_all(blocks_out, ('px', 'py'), split_axis=0, concat_axis=0, til...  94.6 us
    pallas_call x1, Pallas kernels, paint(): pl.pallas_call(paint_kernel, out_shape=jax.ShapeDtypeStruct((rows, LANES)...  79.9 us
    all_to_all x6, starting transfers between devices, exchange(): lax.all_to_all(blocks_out, ('px', 'py'), split_axis=0, concat_axis=0, til...  45.7 us
    reshape x6, local copies, waits for them, and re-layouts, exchange(): blocks_out = blocks_out.reshape(devices_all, -1, LANES)  30 us
    all_gather x1, blocking collectives, on_device(): slab = lax.all_gather(sent, 'py', axis=1, tiled=True)  15.9 us
    reshape x4, local copies, waits for them, and re-layouts, backward(): term = product('ka,zk->az', part.reshape(-1, area), waves)  15.8 us
  transfers between devices with their start and end apart: 12, of which 8 were waited for; matrix products, arithmetic and copies ran while one was open for 36% of the time, Pallas kernels for 13%

profile of v2, /device:TPU:0, one launch (start us, length us, event | category | flops | bytes accessed | tf_op | source)
XLA Modules:
  0.0 626.9 jit_solution(7348791708240856138)
XLA Ops:
  2.3 15.9 %all_gather.3 = f32[2,256,128]{2,1,0:T(8,128)S(1)} all-gather(f32[2,32,128]{2,1,0:T(8,128)S(1)} %pad_maximum_fusion), channel_id=1, replica_groups=mesh['px'=4,'py'=8] {'py'}, dimensions={1}, use_global_device_ids=true | all-gather | bytes 294912 | tf_op jit(solution)/shard_map/all_gather | solution.py:141
  26.5 7.9 %fusion.157 = f32[256,4608]{1,0:T(8,128)} fusion(f32[384,256]{1,0:T(8,128)S(1)} %copy-done.5, f32[4608,384]{1,0:T(8,128)S(1)} %bitcast.219), kind=kOutput, calls=%fused_computation.229 | convolution fusion | flops 2717908992 | bytes 12189696 | tf_op jit(solution)/shard_map/az,zk->ka/dot_general | solution.py:16
  45.3 10.3 %compare_select_fusion = f32[8,384,384]{2,1,0:T(8,128)} fusion(f32[384]{0:T(512)S(1)} %fusion.154, f32[8,384]{1,0:T(8,128)S(1)} %broadcast_add_fusion), kind=kLoop, calls=%fused_computation.12 | loop fusion | flops 58982400 | bytes 4732416 | tf_op jit(solution)/shard_map/jit(_where)/select_n | solution.py:52
  57.0 6.7 %fusion.156 = f32[128,4608]{1,0:T(8,128)S(1)} fusion(f32[384,128]{1,0:T(8,128)S(1)} %copy-done.10, f32[4608,384]{1,0:T(8,128)} %bitcast.220), kind=kOutput, calls=%fused_computation.228 | convolution fusion | flops 1358954496 | bytes 9633792 | tf_op jit(solution)/shard_map/az,zk->ka/dot_general | solution.py:16
  63.7 79.9 %paint.1 = f32[18432,128]{1,0:T(8,128)S(1)} custom-call(s32[256,128]{1,0:T(8,128)S(1)} %get-tuple-element.34.key, f32[256,128]{1,0:T(8,128)S(1)} %slice_bitcast_fusion.weight, s32[256]{0:T(256)S(1)} %get-tuple-element.33.count, f32[768,128]{1,0:T(8,128)S(1)} %select_maximum_fusion.waves), custom_call_target="tpu_custom_call" | custom-call | flops 80000000000 | bytes 9437184 | tf_op jit(solution)/shard_map/paint/pallas_call | solution.py:89
  155.6 7.2 %reshape.174 = f32[4,8,8,48,96]{4,3,2,1,0:T(8,128)} reshape(f32[32,288,128]{2,1,0:T(8,128)} %all-to-all-done) | data formatting | bytes 9437184 | tf_op jit(solution)/shard_map/reshape | solution.py:197
  162.8 7.9 %fusion.3 = f32[8,8,48,384,1]{3,2,0,1,4:T(8,128)S(1)} fusion(f32[4,96,384,1,1]{2,1,3,4,0:T(8,128)S(1)} %copy-done.9, f32[4,8,8,48,96]{4,3,2,1,0:T(8,128)} %reshape.174), kind=kOutput, calls=%fused_computation.10 | convolution fusion | flops 2717908992 | bytes 10027008 | tf_op jit(solution)/shard_map/iqklx,ixn->qkln/dot_general | solution.py:16
  188.5 7.9 %reshape.175 = f32[32,288,128]{2,1,0:T(8,128)} reshape(f32[4,8,8,48,96]{4,3,2,1,0:T(8,128)} %copy.17) | data formatting | bytes 9437184 | tf_op jit(solution)/shard_map/reshape | solution.py:152
  196.4 14.8 %all-to-all-done.1 = f32[32,144,128]{2,1,0:T(8,128)} async-done(((f32[32,144,128]{2,1,0:T(8,128)}), f32[32,144,128]{2,1,0:T(8,128)}, u32[]{:S(2)}, u32[]{:S(2)}) %all-to-all-start.1) | async-done | bytes 2359328 | tf_op jit(solution)/shard_map/all_to_all | solution.py:155
  214.8 9.7 %copy.14 = f32[48,128,384]{2,1,0:T(8,128)} copy(f32[48,128,384]{1,2,0:T(8,128)} %bitcast.218) | data formatting | bytes 18874368 | tf_op jit(solution)/shard_map/ayc,ym->acm/dot_general | solution.py:16
  224.5 11.9 %fusion = f32[96,4,12,384]{3,2,1,0:T(8,128)S(1)} fusion(f32[384,384,1,1]{1,0,3,2:T(8,128)S(1)} %copy-done.12, f32[96,4,16,384]{3,2,1,0:T(8,128)} %bitcast.225), kind=kOutput, calls=%fused_computation | convolution fusion | flops 4076863488 | bytes 17104896 | tf_op jit(solution)/shard_map/ayc,ym->acm/dot_general | solution.py:16
  271.0 50.0 %all-to-all-done.2 = f32[32,288,128]{2,1,0:T(8,128)} async-done(((f32[32,288,128]{2,1,0:T(8,128)}), f32[32,288,128]{2,1,0:T(8,128)}, u32[]{:S(2)}, u32[]{:S(2)}) %all-to-all-start.2) | async-done | bytes 4718624 | tf_op jit(solution)/shard_map/all_to_all | solution.py:155
  334.9 44.2 %collective-permute-done.2 = f32[8,96,384]{2,0,1:T(8,128)} collective-permute-done((f32[8,96,384]{2,0,1:T(8,128)}, f32[8,96,384]{2,0,1:T(8,128)}, u32[]{:S(2)}, u32[]{:S(2)}) %collective-permute-start.2) | collective-permute-done | bytes 1179680 | tf_op jit(solution)/shard_map/ppermute | solution.py:221
  388.0 10.4 %fusion.32 = f32[8,384,8,48]{1,3,0,2:T(8,128)} fusion(f32[8,48,384,1]{2,1,3,0:T(8,128)S(1)} %copy-done.3, f32[8,384,384]{2,1,0:T(8,128)S(1)} %bitcast.224, f32[8,384,384]{2,1,0:T(8,128)S(1)} %fusion.91, f32[8,384,384]{2,1,0:T(8,128)} %fusion.93, f32[8,384,384]{2,1,0:T(8,128)S(1)} %fusion.97, f32[8,384,384]{2,1,0:T(8,128)S(1)} %fusion.95), kind=kOutput, calls=%fused_computation.48 | convolution fusion | flops 2722627584 | bytes 28901376 | tf_op jit(solution)/shard_map/kmn,qlm->qkln/dot_general | solution.py:16
  398.5 7.3 %fusion.43 = f32[4,8,8,48,96]{4,3,0,2,1:T(8,128)S(1)} fusion(f32[4,96,384,1,1]{2,1,0,4,3:T(8,128)S(1)} %copy-done.4, f32[8,384,8,48]{1,3,0,2:T(8,128)} %fusion.32), kind=kOutput, calls=%fused_computation.75 | convolution fusion | flops 2717908992 | bytes 10027008 | tf_op jit(solution)/shard_map/qkln,ixn->iqklx/dot_general | solution.py:16
  409.3 7.9 %reshape.169 = f32[32,288,128]{2,1,0:T(8,128)} reshape(f32[4,8,8,48,96]{4,3,2,1,0:T(8,128)} %copy.15) | data formatting | bytes 9437184 | tf_op jit(solution)/shard_map/reshape | solution.py:152
  417.2 25.4 %all-to-all-start.4 = ((f32[32,288,128]{2,1,0:T(8,128)}), f32[32,288,128]{2,1,0:T(8,128)}, u32[]{:S(2)}, u32[]{:S(2)}) async-start(f32[32,288,128]{2,1,0:T(8,128)} %reshape.169), calls=%async_computation.4 | async-start | bytes 9437184 | tf_op jit(solution)/shard_map/all_to_all | solution.py:155
  451.3 61.3 %collective-permute-done.4 = f32[4,96,384]{2,0,1:T(4,128)S(1)} collective-permute-done((f32[4,96,384]{2,0,1:T(4,128)S(1)}, f32[4,96,384]{2,0,1:T(4,128)S(1)}, u32[]{:S(2)}, u32[]{:S(2)}) %collective-permute-start.4) | collective-permute-done | bytes 589856 | tf_op jit(solution)/shard_map/ppermute | solution.py:221
  526.9 21.9 %all-to-all-done.4 = f32[32,288,128]{2,1,0:T(8,128)} async-done(((f32[32,288,128]{2,1,0:T(8,128)}), f32[32,288,128]{2,1,0:T(8,128)}, u32[]{:S(2)}, u32[]{:S(2)}) %all-to-all-start.4) | async-done | bytes 4718624 | tf_op jit(solution)/shard_map/all_to_all | solution.py:155
  557.1 12.8 %fusion.159 = f32[4608,384]{1,0:T(8,128)} fusion(f32[256,4608]{1,0:T(8,128)} %reshape.179, f32[384,256]{1,0:T(8,128)S(1)} %copy-done.6), kind=kOutput, calls=%fused_computation.231 | convolution fusion | flops 2717908992 | bytes 12189696 | tf_op jit(solution)/shard_map/ka,zk->az/dot_general | solution.py:16
  572.9 10.7 %fusion.2 = f32[4608,384]{1,0:T(8,128)} fusion(f32[4608,384]{1,0:T(8,128)} %fusion.159, f32[128,4608]{1,0:T(8,128)} %reshape.180, f32[384,128]{1,0:T(8,128)S(1)} %copy-done.11), kind=kOutput, calls=%fused_computation.4 | convolution fusion | flops 1362493440 | bytes 16711680 | tf_op jit(solution)/shard_map/ka,zk->az/dot_general | solution.py:16
  589.3 12.7 %fusion.158 = f32[4608,384]{1,0:T(8,128)} fusion(f32[256,4608]{1,0:T(8,128)} %reshape.176, f32[384,256]{1,0:T(8,128)S(1)} %copy-done.6), kind=kOutput, calls=%fused_computation.230 | convolution fusion | flops 2717908992 | bytes 12189696 | tf_op jit(solution)/shard_map/ka,zk->az/dot_general | solution.py:16
  609.2 10.4 %divide_clamp_fusion = f32[4608,384]{1,0:T(8,128)S(1)} fusion(f32[4608,384]{1,0:T(8,128)} %fusion.2, f32[4608,384]{1,0:T(8,128)} %fusion.158, f32[128,4608]{1,0:T(8,128)} %reshape.178, f32[384,128]{1,0:T(8,128)S(1)} %copy-done.11), kind=kOutput, calls=%fused_computation.6 | convolution fusion | flops 1364262912 | bytes 23789568 | tf_op jit(solution)/shard_map/ka,zk->az/dot_general | solution.py:16
  619.6 7.1 %copy.69 = f32[48,96,384]{2,0,1:T(8,128)} copy(f32[48,96,384]{2,1,0:T(8,128)S(1)} %bitcast.226) | data formatting | bytes 14155776 | tf_op jit(solution)/shard_map/reshape | solution.py:251
  (105 shorter events, 164.1 us)
Async XLA Ops:
  18.2 8.3 %copy-start.5 = (f32[384,256]{1,0:T(8,128)S(1)}, f32[384,256]{1,0:T(8,128)}, u32[]{:S(2)}) copy-start(f32[384,256]{1,0:T(8,128)} %constant.230.clone) | copy-start | bytes 1179652
  39.4 112.0 %all-to-all-start = ((f32[32,288,128]{2,1,0:T(8,128)}), f32[32,288,128]{2,1,0:T(8,128)}, u32[]{:S(2)}, u32[]{:S(2)}) async-start(f32[32,288,128]{2,1,0:T(8,128)} %reshape.171), calls=%async_computation | async-start | bytes 9437184 | tf_op jit(solution)/shard_map/all_to_all | solution.py:155
  45.2 11.8 %copy-start.10 = (f32[384,128]{1,0:T(8,128)S(1)}, f32[384,128]{1,0:T(8,128)}, u32[]{:S(2)}) copy-start(f32[384,128]{1,0:T(8,128)} %constant.231.clone) | copy-start | bytes 589828
  151.4 59.8 %all-to-all-start.1 = ((f32[32,144,128]{2,1,0:T(8,128)}), f32[32,144,128]{2,1,0:T(8,128)}, u32[]{:S(2)}, u32[]{:S(2)}) async-start(f32[32,144,128]{2,1,0:T(8,128)} %reshape.170), calls=%async_computation.1 | async-start | bytes 4718592 | tf_op jit(solution)/shard_map/all_to_all | solution.py:155
  155.6 7.2 %copy-start.9 = (f32[4,96,384,1,1]{2,1,3,4,0:T(8,128)S(1)}, f32[4,96,384,1,1]{2,1,3,4,0:T(8,128)}, u32[]{:S(2)}) copy-start(f32[4,96,384,1,1]{2,1,3,4,0:T(8,128)} %constant.244) | copy-start | bytes 1769476
  155.6 19.3 %slice-start = ((s8[4718592]{0:T(1024)(128)(4,1)}), s8[524288]{0:T(1024)(128)(4,1)S(1)}, s32[]{:S(2)}) async-start(s8[4718592]{0:T(1024)(128)(4,1)} %bitcast.221), calls=%async_computation.6 | async-start | bytes 1048576
  162.8 7.9 %copy-start.3 = (f32[8,48,384,1]{2,1,3,0:T(8,128)S(1)}, f32[8,48,384,1]{2,1,3,0:T(8,128)}, u32[]{:S(2)}) copy-start(f32[8,48,384,1]{2,1,3,0:T(8,128)} %constant.242) | copy-start | bytes 1769476
  162.8 12.1 %slice-start.1 = ((s8[4718592]{0:T(1024)(128)(4,1)}), s8[4194304]{0:T(1024)(128)(4,1)S(1)}, s32[]{:S(2)}) async-start(s8[4718592]{0:T(1024)(128)(4,1)} %bitcast.221), calls=%async_computation.7 | async-start | bytes 8388608
  211.2 109.8 %all-to-all-start.2 = ((f32[32,288,128]{2,1,0:T(8,128)}), f32[32,288,128]{2,1,0:T(8,128)}, u32[]{:S(2)}, u32[]{:S(2)}) async-start(f32[32,288,128]{2,1,0:T(8,128)} %reshape.175), calls=%async_computation.2 | async-start | bytes 9437184 | tf_op jit(solution)/shard_map/all_to_all | solution.py:155
  214.8 9.7 %copy-start.12 = (f32[384,384,1,1]{1,0,3,2:T(8,128)S(1)}, f32[384,384,1,1]{1,0,3,2:T(8,128)}, u32[]{:S(2)}) copy-start(f32[384,384,1,1]{1,0,3,2:T(8,128)} %constant.241) | copy-start | bytes 1769476
  236.4 5.1 copy-start.2
  241.5 89.8 %collective-permute-start = (f32[8,96,384]{2,0,1:T(8,128)}, f32[8,96,384]{2,0,1:T(8,128)}, u32[]{:S(2)}, u32[]{:S(2)}) collective-permute-start(f32[8,96,384]{2,0,1:T(8,128)} %get-tuple-element.29), channel_id=1, source_target_pairs={{0,8},{8,16},{16,24},{24,0},{1,9},{9,17},{17,25},{25,1},{2,10},{10... | collective-permute-start | bytes 3538952 | tf_op jit(solution)/shard_map/ppermute | solution.py:221
  321.0 96.2 %all-to-all-start.3 = ((f32[32,144,128]{2,1,0:T(8,128)}), f32[32,144,128]{2,1,0:T(8,128)}, u32[]{:S(2)}, u32[]{:S(2)}) async-start(f32[32,144,128]{2,1,0:T(8,128)} %reshape.173), calls=%async_computation.3 | async-start | bytes 4718592 | tf_op jit(solution)/shard_map/all_to_all | solution.py:155
  324.7 54.4 %collective-permute-start.2 = (f32[8,96,384]{2,0,1:T(8,128)}, f32[8,96,384]{2,0,1:T(8,128)}, u32[]{:S(2)}, u32[]{:S(2)}) collective-permute-start(f32[8,96,384]{2,0,1:T(8,128)} %get-tuple-element.30), channel_id=1, source_target_pairs={{0,24},{8,0},{16,8},{24,16},{1,25},{9,1},{17,9},{25,17},{2,26},{10... | collective-permute-start | bytes 3538952 | tf_op jit(solution)/shard_map/ppermute | solution.py:221
  327.3 55.2 %collective-permute-start.1 = (f32[8,96,384]{2,0,1:T(8,128)}, f32[8,96,384]{2,0,1:T(8,128)}, u32[]{:S(2)}, u32[]{:S(2)}) collective-permute-start(f32[8,96,384]{2,0,1:T(8,128)} %get-tuple-element.31), channel_id=1, source_target_pairs={{0,16},{8,24},{16,0},{24,8},{1,17},{9,25},{17,1},{25,9},{2,18},{10... | collective-permute-start | bytes 3538952 | tf_op jit(solution)/shard_map/ppermute | solution.py:221
  331.3 56.7 %slice-start.2 = ((s8[4718592]{0:T(1024)(128)(4,1)}), s8[4194304]{0:T(1024)(128)(4,1)S(1)}, s32[]{:S(2)}) async-start(s8[4718592]{0:T(1024)(128)(4,1)} %bitcast.223), calls=%async_computation.8 | async-start | bytes 8388608
  334.9 53.1 %slice-start.3 = ((s8[4718592]{0:T(1024)(128)(4,1)}), s8[524288]{0:T(1024)(128)(4,1)S(1)}, s32[]{:S(2)}) async-start(s8[4718592]{0:T(1024)(128)(4,1)} %bitcast.223), calls=%async_computation.9 | async-start | bytes 1048576
  417.2 131.6 %all-to-all-start.4 = ((f32[32,288,128]{2,1,0:T(8,128)}), f32[32,288,128]{2,1,0:T(8,128)}, u32[]{:S(2)}, u32[]{:S(2)}) async-start(f32[32,288,128]{2,1,0:T(8,128)} %reshape.169), calls=%async_computation.4 | async-start | bytes 9437184 | tf_op jit(solution)/shard_map/all_to_all | solution.py:155
  442.6 7.6 %copy-start.8 = (f32[4,96,384]{2,1,0:T(8,128)S(1)}, f32[4,96,384]{2,1,0:T(8,128)}, u32[]{:S(2)}) copy-start(f32[4,96,384]{2,1,0:T(8,128)} %constant.239) | copy-start | bytes 1769476
  445.3 67.2 %collective-permute-start.4 = (f32[4,96,384]{2,0,1:T(4,128)S(1)}, f32[4,96,384]{2,0,1:T(4,128)S(1)}, u32[]{:S(2)}, u32[]{:S(2)}) collective-permute-start(f32[4,96,384]{2,0,1:T(4,128)S(1)} %get-tuple-element.27), channel_id=1, source_target_pairs={{0,16},{8,24},{16,0},{24,8},{1,17},{9,25},{17,1},{25,9},{2,18},{10... | collective-permute-start | bytes 1769480 | tf_op jit(solution)/shard_map/ppermute | solution.py:221
  447.1 70.4 %collective-permute-start.3 = (f32[4,96,384]{2,0,1:T(4,128)S(1)}, f32[4,96,384]{2,0,1:T(4,128)S(1)}, u32[]{:S(2)}, u32[]{:S(2)}) collective-permute-start(f32[4,96,384]{2,0,1:T(4,128)S(1)} %get-tuple-element.25), channel_id=1, source_target_pairs={{0,8},{8,16},{16,24},{24,0},{1,9},{9,17},{17,25},{25,1},{2,10},{10... | collective-permute-start | bytes 1769480 | tf_op jit(solution)/shard_map/ppermute | solution.py:221
  448.6 67.8 %collective-permute-start.5 = (f32[4,96,384]{2,0,1:T(4,128)S(1)}, f32[4,96,384]{2,0,1:T(4,128)S(1)}, u32[]{:S(2)}, u32[]{:S(2)}) collective-permute-start(f32[4,96,384]{2,0,1:T(4,128)S(1)} %get-tuple-element.26), channel_id=1, source_target_pairs={{0,24},{8,0},{16,8},{24,16},{1,25},{9,1},{17,9},{25,17},{2,26},{10... | collective-permute-start | bytes 1769480 | tf_op jit(solution)/shard_map/ppermute | solution.py:221
  548.8 58.6 %all-to-all-start.5 = ((f32[32,144,128]{2,1,0:T(8,128)}), f32[32,144,128]{2,1,0:T(8,128)S(1)}, u32[]{:S(2)}, u32[]{:S(2)}) async-start(f32[32,144,128]{2,1,0:T(8,128)} %reshape.177), calls=%async_computation.5 | async-start | bytes 4718592 | tf_op jit(solution)/shard_map/all_to_all | solution.py:155
  551.8 5.4 copy-start.6
  (5 other events, 17.4 us)

commit v3 on v2

--- a/solution.py
+++ b/solution.py
@@ -10,6 +10,7 @@
 LANES = 128
 UNROLL = 8
 TAB_BITS = 10
+SUBLANES = 8
 
 
 def product(form, left, right):
@@ -100,6 +101,164 @@
     )(key, weight, count, waves)
 
 
+def halves(values):
+    high = values.astype(jnp.bfloat16)
+    return high, (values - high.astype(jnp.float32)).astype(jnp.bfloat16)
+
+
+def split_table(values):
+    high = values.astype(jnp.bfloat16)
+    return high, (values - np.asarray(high, np.float32)).astype(jnp.bfloat16)
+
+
+def thrice(left, right, contract):
+    form = ((contract, contract), ((), ()))
+    (high_l, low_l), (high_r, low_r) = left, right
+
+    def once(one, other):
+        return lax.dot_general(one, other, form, preferred_element_type=jnp.float32)
+
+    return once(high_l, high_r) + (once(high_l, low_r) + once(low_l, high_r))
+
+
+def spread_kernel(high, low, density, out, rows):
+    rows_x, deep, grid = density.shape
+    tiles = rows_x * deep // LANES
+    count = high.shape[0]
+    stride = out.shape[0] // count
+    flat = density[...].reshape(rows_x * deep, grid)
+    for tile in range(grid // LANES):
+        rows[tile] = flat[:, tile * LANES : (tile + 1) * LANES]
+    lines = jnp.concatenate(
+        [
+            jnp.concatenate(
+                [rows[tile, pl.ds(y, rows_x, stride=deep), :] for y in range(deep)]
+            )
+            for tile in range(grid // LANES)
+        ],
+        axis=1,
+    )
+    spec = thrice((high[...], low[...]), halves(lines), (1,))
+    for tile in range(tiles):
+        spot = pl.program_id(0) * tiles + tile
+        out[pl.ds(spot, count, stride=stride), :] = spec[:, tile * LANES : (tile + 1) * LANES]
+
+
+def spread(density, waves):
+    rows_x, rows_y, grid = density.shape
+    high, low = split_table(np.ascontiguousarray(waves.T))
+    count = high.shape[0]
+    return pl.pallas_call(
+        spread_kernel,
+        grid=(rows_y // SUBLANES,),
+        out_shape=jax.ShapeDtypeStruct((count * rows_x * rows_y // LANES, LANES), jnp.float32),
+        in_specs=[
+            pl.BlockSpec((count, grid), lambda i: (0, 0)),
+            pl.BlockSpec((count, grid), lambda i: (0, 0)),
+            pl.BlockSpec((rows_x, SUBLANES, grid), lambda i: (0, i, 0)),
+        ],
+        out_specs=pl.BlockSpec((count * rows_x * rows_y // LANES, LANES), lambda i: (0, 0)),
+        scratch_shapes=[pltpu.VMEM((grid // LANES, rows_x * SUBLANES, LANES), jnp.float32)],
+        cost_estimate=pl.CostEstimate(
+            flops=6 * count * grid * rows_x * rows_y,
+            bytes_accessed=4 * rows_x * rows_y * (grid + count),
+            transcendentals=0,
+        ),
+        compiler_params=pltpu.CompilerParams(vmem_limit_bytes=40 << 20),
+        name="spread",
+    )(jnp.asarray(high), jnp.asarray(low), density)
+
+
+def finish_kernel(high, low, last, photon, density, out, rows):
+    rows_x, deep, grid = out.shape
+    tiles = rows_x * deep // LANES
+    count = high.shape[0]
+    stride = last.shape[0] // count
+    spec = jnp.concatenate(
+        [
+            last[pl.ds(pl.program_id(0) * tiles + tile, count, stride=stride), :]
+            for tile in range(tiles)
+        ],
+        axis=1,
+    )
+    field = thrice(halves(spec), (high[...], low[...]), (0,)) + photon[...]
+    fraction = jnp.clip(field / jnp.maximum(density[...], 0.5), 0.0, 1.0)
+    for tile in range(grid // LANES):
+        lanes = slice(tile * LANES, (tile + 1) * LANES)
+        for y in range(deep):
+            rows[tile, pl.ds(y, rows_x, stride=deep), :] = fraction[
+                y * rows_x : (y + 1) * rows_x, lanes
+            ]
+        out[:, :, lanes] = rows[tile].reshape(rows_x, deep, LANES)
+
+
+def finish(last, photon, density, waves, rows_x, rows_y):
+    grid = photon.shape[1]
+    high, low = split_table(np.ascontiguousarray(waves.T))
+    count = high.shape[0]
+    last = last.reshape(-1, LANES)
+    share = rows_x * SUBLANES
+    return pl.pallas_call(
+        finish_kernel,
+        grid=(rows_y // SUBLANES,),
+        out_shape=jax.ShapeDtypeStruct((rows_x, rows_y, grid), jnp.float32),
+        in_specs=[
+            pl.BlockSpec((count, grid), lambda i: (0, 0)),
+            pl.BlockSpec((count, grid), lambda i: (0, 0)),
+            pl.BlockSpec(last.shape, lambda i: (0, 0)),
+            pl.BlockSpec((share, grid), lambda i: (i, 0)),
+            pl.BlockSpec((share, grid), lambda i: (i, 0)),
+        ],
+        out_specs=pl.BlockSpec((rows_x, SUBLANES, grid), lambda i: (0, i, 0)),
+        scratch_shapes=[pltpu.VMEM((grid // LANES, share, LANES), jnp.float32)],
+        cost_estimate=pl.CostEstimate(
+            flops=6 * count * grid * rows_x * rows_y,
+            bytes_accessed=4 * rows_x * rows_y * (3 * grid + count),
+            transcendentals=0,
+        ),
+        compiler_params=pltpu.CompilerParams(vmem_limit_bytes=40 << 20),
+        name="finish",
+    )(jnp.asarray(high), jnp.asarray(low), last, photon, density)
+
+
+def gather_kernel(mine, everyone, send_sems, receive_sems):
+    count = everyone.shape[0]
+    me = lax.axis_index("py")
+    barrier = pltpu.get_barrier_semaphore()
+    for shift in range(1, count):
+        pl.semaphore_signal(
+            barrier, inc=1, device_id={"py": lax.rem(me + shift, count)},
+            device_id_type=pl.DeviceIdType.MESH,
+        )
+    pl.semaphore_wait(barrier, count - 1)
+    copies = [
+        pltpu.make_async_remote_copy(
+            mine, everyone.at[me], send_sems.at[shift], receive_sems.at[shift],
+            device_id={"py": lax.rem(me + shift, count)},
+            device_id_type=pl.DeviceIdType.MESH,
+        )
+        for shift in range(1, count)
+    ]
+    for copy in copies:
+        copy.start()
+    everyone[pl.ds(me, 1)] = mine[...][None]
+    for copy in copies:
+        copy.wait()
+
+
+def gather(mine, count):
+    vmem = pl.BlockSpec(memory_space=pltpu.VMEM)
+    return pl.pallas_call(
+        gather_kernel,
+        out_shape=jax.ShapeDtypeStruct((count,) + mine.shape, mine.dtype),
+        in_specs=[vmem],
+        out_specs=vmem,
+        scratch_shapes=[pltpu.SemaphoreType.DMA((count,)), pltpu.SemaphoreType.DMA((count,))],
+        compiler_params=pltpu.CompilerParams(collective_id=0, has_side_effects=True),
+        name="gather",
+    )(mine)
+
+
 def on_device(photons, halo_cells, halo_counts, owners, density):
     rows_x, rows_y, grid = density.shape
     slots = photons.shape[1]
@@ -116,12 +275,10 @@
     table_y = table.reshape(count_y, rows_y, grid)
 
     first = max(1, planes * 2 // 3)
-    parts = [(0, first)] + ([(first, planes)] if first < planes else [])
+    assert first < planes
+    parts = [(0, first), (first, planes)]
     by_plane = table_np.reshape(grid, devices_all, planes)
-    tables = [
-        jnp.asarray(np.ascontiguousarray(by_plane[:, :, a:b]).reshape(grid, devices_all * (b - a)))
-        for a, b in parts
-    ]
+    tables = [by_plane[:, :, a:b].reshape(grid, devices_all * (b - a)) for a, b in parts]
 
     pair = LANES // 2
     width = pair // count_x
@@ -137,8 +294,9 @@
     cell_z = halo_cells % grid
     row = (cell_x // 2) * grid + cell_y
     key = jnp.where(live, row * (2 * grid) + (cell_x % 2) * grid + cell_z, 0)
-    sent = jnp.stack([weights, key.astype(jnp.float32)])
-    slab = lax.all_gather(sent, "py", axis=1, tiled=True)
+    sent = jnp.concatenate([weights, key.astype(jnp.float32)])
+    slab = gather(sent, count_y).reshape(count_y, 2, -1, slots)
+    slab = [slab[:, kind].reshape(-1, slots) for kind in range(2)]
     slab, density = lax.optimization_barrier((slab, density))
 
     def signed(index_values):
@@ -158,8 +316,7 @@
         received.append(got)
         return got
 
-    density_rows = density.transpose(1, 0, 2).reshape(area, grid)
-    specs = [product("az,zk->ka", density_rows, part) for part in tables]
+    specs = [spread(density, part) for part in tables]
     density_got = [exchange(specs[0])]
 
     freq = signed(jnp.arange(grid, dtype=jnp.int32))
@@ -240,15 +397,15 @@
     def backward(got):
         total = None
         for part, waves in zip(got, tables):
-            term = product("ka,zk->az", part.reshape(-1, area), waves)
+            term = product("ka,zk->az", part.reshape(-1, area), jnp.asarray(waves))
             total = term if total is None else total + term
         return total
 
     density_smooth = backward(density_back)
-    photon_smooth = backward(photon_back)
-
-    fraction = jnp.clip(photon_smooth / jnp.maximum(density_smooth, 0.5), 0.0, 1.0)
-    return fraction.reshape(rows_y, rows_x, grid).transpose(1, 0, 2)
+    photon_smooth = backward(photon_back[:-1])
+    return finish(
+        photon_back[-1], photon_smooth, density_smooth, tables[-1], rows_x, rows_y
+    )
 
 
 def solution(mesh):

time: 637 us -> 623 us (0.978)
  Pallas kernels: 79.9 us -> 114 us
  matrix products: 151 us -> 125 us
  waiting for transfers between devices: 203 us -> 226 us
  starting transfers between devices: 55.2 us -> 36 us
  blocking collectives: 15.9 us -> 0 us
  local copies, waits for them, and re-layouts: 104 us -> 94.4 us
    pallas_call x0 -> x4, Pallas kernels: none -> 33.8 us  [the longest x2 12.7 us: spread(): pl.pallas_call(spread_kernel, grid=(rows_y // SUBLANES,), out_shape=jax.S...]
    ppermute x6, waiting for transfers between devices: 108 us -> 134 us  [around(): lax.ppermute(block, 'px', [(i, (i + shift) % count_x) for i in range(coun...]
    dot_general x27 -> x24, matrix products: 151 us -> 125 us  [product(): return jnp.einsum(form, left, right, precision=lax.Precision.HIGH)]
    all_to_all x6, starting transfers between devices: 45.7 us -> 26.2 us  [exchange(): lax.all_to_all(blocks_out, ('px', 'py'), split_axis=0, concat_axis=0, til...]
    all_gather x1 -> x0, blocking collectives: 15.9 us -> none  [on_device(): slab = lax.all_gather(sent, 'py', axis=1, tiled=True)]
    unnamed x34 -> x48, local copies, waits for them, and re-layouts: 9.06 us -> 19.1 us
    reshape x5 -> x3, local copies, waits for them, and re-layouts: 22.9 us -> 13.8 us  [backward(): term = product('ka,zk->az', part.reshape(-1, area), jnp.asarray(waves))]
    reshape x6 -> x4, local copies, waits for them, and re-layouts: 30 us -> 23.4 us  [exchange(): blocks_out = blocks_out.reshape(devices_all, -1, LANES)]
  transfers between devices with their start and end apart: 12 -> 12, of which waited for: 8 -> 8; matrix products, arithmetic and copies ran while one was open for 36% -> 35% of each run, Pallas kernels for 13% -> 14%
where the time goes in v3:
time: 623 us; the launch traced here: 615 us
  waiting for transfers between devices  226 us (36%)
  matrix products  125 us (20%)
  Pallas kernels  114 us (18%)
  local copies, waits for them, and re-layouts  94.4 us (15%)
  starting transfers between devices  36 us (6%)
  other arithmetic  18.1 us (3%)
    ppermute x6, waiting for transfers between devices, around(): lax.ppermute(block, 'px', [(i, (i + shift) % count_x) for i in range(coun...  134 us
    dot_general x24, matrix products, product(): return jnp.einsum(form, left, right, precision=lax.Precision.HIGH)  125 us
    all_to_all x6, waiting for transfers between devices, exchange(): lax.all_to_all(blocks_out, ('px', 'py'), split_axis=0, concat_axis=0, til...  92.4 us
    pallas_call x1, Pallas kernels, paint(): pl.pallas_call(paint_kernel, out_shape=jax.ShapeDtypeStruct((rows, LANES)...  79.9 us
    all_to_all x6, starting transfers between devices, exchange(): lax.all_to_all(blocks_out, ('px', 'py'), split_axis=0, concat_axis=0, til...  26.2 us
    reshape x4, local copies, waits for them, and re-layouts, exchange(): blocks_out = blocks_out.reshape(devices_all, -1, LANES)  23.4 us
    unnamed x48, local copies, waits for them, and re-layouts  19.1 us
    select_n x2, other arithmetic, top_hat(): return jnp.where(radial > 0, value, 1.0)  14.7 us
  transfers between devices with their start and end apart: 12, of which 8 were waited for; matrix products, arithmetic and copies ran while one was open for 35% of the time, Pallas kernels for 14%

profile of v3, /device:TPU:0, one launch (start us, length us, event | category | flops | bytes accessed | tf_op | source)
XLA Modules:
  0.0 615.1 jit_solution(1317385844985350608)
XLA Ops:
  2.9 11.7 %gather.1 = f32[8,64,128]{2,1,0:T(8,128)} custom-call(f32[64,128]{1,0:T(8,128)} %pad_maximum_fusion.mine), custom_call_target="tpu_custom_call" | custom-call | tf_op jit(solution)/shard_map/gather/pallas_call | solution.py:251
  20.4 6.0 spread.3
  28.6 6.5 %all-to-all-start = ((f32[32,288,128]{2,1,0:T(8,128)}), f32[32,288,128]{2,1,0:T(8,128)}, u32[]{:S(2)}, u32[]{:S(2)}) async-start(f32[32,288,128]{2,1,0:T(8,128)} %bitcast.189), calls=%async_computation | async-start | bytes 9437184 | tf_op jit(solution)/shard_map/all_to_all | solution.py:313
  36.4 10.2 %compare_select_fusion = f32[8,384,384]{2,1,0:T(8,128)} fusion(f32[384]{0:T(512)S(1)} %fusion.154, f32[8,384]{1,0:T(8,128)S(1)} %broadcast_add_fusion), kind=kLoop, calls=%fused_computation.8 | loop fusion | flops 58982400 | bytes 4732416 | tf_op jit(solution)/shard_map/jit(_where)/select_n | solution.py:53
  49.8 6.7 %spread.2 = f32[4608,128]{1,0:T(8,128)} custom-call(bf16[128,384]{1,0:T(8,128)(2,1)S(1)} %copy-done.5, bf16[128,384]{1,0:T(8,128)(2,1)S(1)} %copy-done.7, f32[96,48,384]{2,1,0:T(8,128)S(1)} %copy-done.2), custom_call_target="tpu_custom_call" | custom-call | flops 1358954496 | bytes 9437184 | tf_op jit(solution)/shard_map/spread/pallas_call | solution.py:151
  56.7 79.9 %paint.1 = f32[18432,128]{1,0:T(8,128)S(1)} custom-call(s32[256,128]{1,0:T(8,128)S(1)} %get-tuple-element.37.key, f32[256,128]{1,0:T(8,128)S(1)} %bitcast.193, s32[256]{0:T(256)S(1)} %get-tuple-element.38.count, f32[768,128]{1,0:T(8,128)S(1)} %select_maximum_fusion.waves), custom_call_target="tpu_custom_call" | custom-call | flops 80000000000 | bytes 9437184 | tf_op jit(solution)/shard_map/paint/pallas_call | solution.py:90
  147.1 7.2 %reshape.164 = f32[4,8,8,48,96]{4,3,2,1,0:T(8,128)} reshape(f32[32,288,128]{2,1,0:T(8,128)} %all-to-all-done) | data formatting | bytes 9437184 | tf_op jit(solution)/shard_map/reshape | solution.py:354
  154.2 8.1 %fusion.2 = f32[8,8,48,384,1]{3,2,0,1,4:T(8,128)S(1)} fusion(f32[4,96,384,1,1]{2,1,3,4,0:T(8,128)S(1)} %copy-done.16, f32[4,8,8,48,96]{4,3,2,1,0:T(8,128)} %reshape.164), kind=kOutput, calls=%fused_computation.6 | convolution fusion | flops 2717908992 | bytes 10027008 | tf_op jit(solution)/shard_map/iqklx,ixn->qkln/dot_general | solution.py:17
  180.2 7.9 %reshape.165 = f32[32,288,128]{2,1,0:T(8,128)} reshape(f32[4,8,8,48,96]{4,3,2,1,0:T(8,128)} %copy.26) | data formatting | bytes 9437184 | tf_op jit(solution)/shard_map/reshape | solution.py:310
  188.1 14.5 %all-to-all-done.1 = f32[32,144,128]{2,1,0:T(8,128)} async-done(((f32[32,144,128]{2,1,0:T(8,128)}), f32[32,144,128]{2,1,0:T(8,128)}, u32[]{:S(2)}, u32[]{:S(2)}) %all-to-all-start.1) | async-done | bytes 2359328 | tf_op jit(solution)/shard_map/all_to_all | solution.py:313
  206.3 9.6 %copy.22 = f32[48,128,384]{2,1,0:T(8,128)} copy(f32[48,128,384]{1,2,0:T(8,128)} %bitcast.191) | data formatting | bytes 18874368 | tf_op jit(solution)/shard_map/ayc,ym->acm/dot_general | solution.py:17
  215.9 11.9 %fusion = f32[96,4,12,384]{3,2,1,0:T(8,128)S(1)} fusion(f32[384,384,1,1]{1,0,3,2:T(8,128)S(1)} %copy-done.18, f32[96,4,16,384]{3,2,1,0:T(8,128)} %bitcast.198), kind=kOutput, calls=%fused_computation | convolution fusion | flops 4076863488 | bytes 17104896 | tf_op jit(solution)/shard_map/ayc,ym->acm/dot_general | solution.py:17
  262.8 50.0 %all-to-all-done.2 = f32[32,288,128]{2,1,0:T(8,128)} async-done(((f32[32,288,128]{2,1,0:T(8,128)}), f32[32,288,128]{2,1,0:T(8,128)}, u32[]{:S(2)}, u32[]{:S(2)}) %all-to-all-start.2) | async-done | bytes 4718624 | tf_op jit(solution)/shard_map/all_to_all | solution.py:313
  326.8 68.1 %collective-permute-done.4 = f32[8,96,384]{2,0,1:T(8,128)} collective-permute-done((f32[8,96,384]{2,0,1:T(8,128)}, f32[8,96,384]{2,0,1:T(8,128)}, u32[]{:S(2)}, u32[]{:S(2)}) %collective-permute-start.4) | collective-permute-done | bytes 1179680 | tf_op jit(solution)/shard_map/ppermute | solution.py:378
  403.9 10.6 %fusion.31 = f32[8,384,8,48]{1,3,0,2:T(8,128)} fusion(f32[8,48,384,1]{2,1,3,0:T(8,128)S(1)} %copy-done.12, f32[8,384,384]{2,1,0:T(8,128)S(1)} %bitcast.197, f32[8,384,384]{2,1,0:T(8,128)S(1)} %fusion.90, f32[8,384,384]{2,1,0:T(8,128)S(1)} %fusion.92, f32[8,384,384]{2,1,0:T(8,128)S(1)} %fusion.96, f32[8,384,384]{2,1,0:T(8,128)} %fusion.94), kind=kOutput, calls=%fused_computation.44 | convolution fusion | flops 2722627584 | bytes 28901376 | tf_op jit(solution)/shard_map/kmn,qlm->qkln/dot_general | solution.py:17
  414.4 7.3 %fusion.42 = f32[4,8,8,48,96]{4,3,0,2,1:T(8,128)S(1)} fusion(f32[4,96,384,1,1]{2,1,0,4,3:T(8,128)S(1)} %copy-done.13, f32[8,384,8,48]{1,3,0,2:T(8,128)} %fusion.31), kind=kOutput, calls=%fused_computation.71 | convolution fusion | flops 2717908992 | bytes 10027008 | tf_op jit(solution)/shard_map/qkln,ixn->iqklx/dot_general | solution.py:17
  425.3 7.9 %reshape.159 = f32[32,288,128]{2,1,0:T(8,128)} reshape(f32[4,8,8,48,96]{4,3,2,1,0:T(8,128)} %copy.24) | data formatting | bytes 9437184 | tf_op jit(solution)/shard_map/reshape | solution.py:310
  445.0 45.3 %collective-permute-done.2 = f32[4,96,384]{2,0,1:T(4,128)S(1)} collective-permute-done((f32[4,96,384]{2,0,1:T(4,128)S(1)}, f32[4,96,384]{2,0,1:T(4,128)S(1)}, u32[]{:S(2)}, u32[]{:S(2)}) %collective-permute-start.2) | collective-permute-done | bytes 589856 | tf_op jit(solution)/shard_map/ppermute | solution.py:378
  492.6 20.5 %collective-permute-done = f32[4,96,384]{2,0,1:T(4,128)S(1)} collective-permute-done((f32[4,96,384]{2,0,1:T(4,128)S(1)}, f32[4,96,384]{2,0,1:T(4,128)S(1)}, u32[]{:S(2)}, u32[]{:S(2)}) %collective-permute-start) | collective-permute-done | bytes 589856 | tf_op jit(solution)/shard_map/ppermute | solution.py:378
  522.6 21.1 %all-to-all-done.4 = f32[32,288,128]{2,1,0:T(8,128)} async-done(((f32[32,288,128]{2,1,0:T(8,128)}), f32[32,288,128]{2,1,0:T(8,128)}, u32[]{:S(2)}, u32[]{:S(2)}) %all-to-all-start.4) | async-done | bytes 4718624 | tf_op jit(solution)/shard_map/all_to_all | solution.py:313
  552.0 12.8 %fusion.158 = f32[4608,384]{1,0:T(8,128)} fusion(f32[256,4608]{1,0:T(8,128)} %reshape.168, f32[384,256]{1,0:T(8,128)S(1)} %copy-done.17), kind=kOutput, calls=%fused_computation.223 | convolution fusion | flops 2717908992 | bytes 12189696 | tf_op jit(solution)/shard_map/ka,zk->az/dot_general | solution.py:17
  567.7 10.5 %convolution_add_fusion.density = f32[4608,384]{1,0:T(8,128)} fusion(f32[4608,384]{1,0:T(8,128)} %fusion.158, f32[128,4608]{1,0:T(8,128)} %reshape.169, f32[384,128]{1,0:T(8,128)S(1)} %copy-done.19), kind=kOutput, calls=%fused_computation.2 | convolution fusion | flops 1360723968 | bytes 16711680 | tf_op jit(solution)/shard_map/ka,zk->az/dot_general | solution.py:17
  583.7 12.8 %fusion.157.photon = f32[4608,384]{1,0:T(8,128)} fusion(f32[256,4608]{1,0:T(8,128)} %reshape.167, f32[384,256]{1,0:T(8,128)S(1)} %copy-done.17), kind=kOutput, calls=%fused_computation.222 | convolution fusion | flops 2717908992 | bytes 12189696 | tf_op jit(solution)/shard_map/ka,zk->az/dot_general | solution.py:17
  605.3 9.4 %finish.1 = f32[96,48,384]{2,1,0:T(8,128)} custom-call(bf16[128,384]{1,0:T(8,128)(2,1)S(1)} %copy-done.6, bf16[128,384]{1,0:T(8,128)(2,1)S(1)} %copy-done.8, f32[4608,128]{1,0:T(8,128)S(1)} %bitcast.190, f32[4608,384]{1,0:T(8,128)S(1)} %copy-done, f32[4608,384]{1,0:T(8,128)} %convolution_add_fusion.density), custom_call_target="tpu_custom_call" | custom-call | flops 1358954496 | bytes 23592960 | tf_op jit(solution)/shard_map/finish/pallas_call | solution.py:201
  (114 shorter events, 157.4 us)
Async XLA Ops:
  28.6 112.7 %all-to-all-start = ((f32[32,288,128]{2,1,0:T(8,128)}), f32[32,288,128]{2,1,0:T(8,128)}, u32[]{:S(2)}, u32[]{:S(2)}) async-start(f32[32,288,128]{2,1,0:T(8,128)} %bitcast.189), calls=%async_computation | async-start | bytes 9437184 | tf_op jit(solution)/shard_map/all_to_all | solution.py:313
  35.2 11.6 %copy-start.5 = (bf16[128,384]{1,0:T(8,128)(2,1)S(1)}, bf16[128,384]{1,0:T(8,128)(2,1)}, u32[]{:S(2)}) copy-start(bf16[128,384]{1,0:T(8,128)(2,1)} %constant.239.clone.high) | copy-start | bytes 294916
  35.2 11.6 %copy-start.7 = (bf16[128,384]{1,0:T(8,128)(2,1)S(1)}, bf16[128,384]{1,0:T(8,128)(2,1)}, u32[]{:S(2)}) copy-start(bf16[128,384]{1,0:T(8,128)(2,1)} %constant.240.clone.low) | copy-start | bytes 294916
  141.4 61.3 %all-to-all-start.1 = ((f32[32,144,128]{2,1,0:T(8,128)}), f32[32,144,128]{2,1,0:T(8,128)}, u32[]{:S(2)}, u32[]{:S(2)}) async-start(f32[32,144,128]{2,1,0:T(8,128)} %bitcast.51), calls=%async_computation.1 | async-start | bytes 4718592 | tf_op jit(solution)/shard_map/all_to_all | solution.py:313
  147.0 7.2 %copy-start.16 = (f32[4,96,384,1,1]{2,1,3,4,0:T(8,128)S(1)}, f32[4,96,384,1,1]{2,1,3,4,0:T(8,128)}, u32[]{:S(2)}) copy-start(f32[4,96,384,1,1]{2,1,3,4,0:T(8,128)} %constant.255) | copy-start | bytes 1769476
  147.1 19.5 %slice-start = ((s8[4718592]{0:T(1024)(128)(4,1)}), s8[524288]{0:T(1024)(128)(4,1)S(1)}, s32[]{:S(2)}) async-start(s8[4718592]{0:T(1024)(128)(4,1)} %bitcast.194), calls=%async_computation.6 | async-start | bytes 1048576
  154.2 8.2 %copy-start.12 = (f32[8,48,384,1]{2,1,3,0:T(8,128)S(1)}, f32[8,48,384,1]{2,1,3,0:T(8,128)}, u32[]{:S(2)}) copy-start(f32[8,48,384,1]{2,1,3,0:T(8,128)} %constant.253) | copy-start | bytes 1769476
  154.2 12.3 %slice-start.1 = ((s8[4718592]{0:T(1024)(128)(4,1)}), s8[4194304]{0:T(1024)(128)(4,1)S(1)}, s32[]{:S(2)}) async-start(s8[4718592]{0:T(1024)(128)(4,1)} %bitcast.194), calls=%async_computation.7 | async-start | bytes 8388608
  202.6 110.2 %all-to-all-start.2 = ((f32[32,288,128]{2,1,0:T(8,128)}), f32[32,288,128]{2,1,0:T(8,128)}, u32[]{:S(2)}, u32[]{:S(2)}) async-start(f32[32,288,128]{2,1,0:T(8,128)} %reshape.165), calls=%async_computation.2 | async-start | bytes 9437184 | tf_op jit(solution)/shard_map/all_to_all | solution.py:313
  206.3 9.7 %copy-start.18 = (f32[384,384,1,1]{1,0,3,2:T(8,128)S(1)}, f32[384,384,1,1]{1,0,3,2:T(8,128)}, u32[]{:S(2)}) copy-start(f32[384,384,1,1]{1,0,3,2:T(8,128)} %constant.252) | copy-start | bytes 1769476
  232.9 90.3 %collective-permute-start.5 = (f32[8,96,384]{2,0,1:T(8,128)}, f32[8,96,384]{2,0,1:T(8,128)}, u32[]{:S(2)}, u32[]{:S(2)}) collective-permute-start(f32[8,96,384]{2,0,1:T(8,128)} %get-tuple-element.28), channel_id=1, source_target_pairs={{0,24},{8,0},{16,8},{24,16},{1,25},{9,1},{17,9},{25,17},{2,26},{10... | collective-permute-start | bytes 3538952 | tf_op jit(solution)/shard_map/ppermute | solution.py:378
  312.8 120.4 %all-to-all-start.3 = ((f32[32,144,128]{2,1,0:T(8,128)}), f32[32,144,128]{2,1,0:T(8,128)}, u32[]{:S(2)}, u32[]{:S(2)}) async-start(f32[32,144,128]{2,1,0:T(8,128)} %reshape.163), calls=%async_computation.3 | async-start | bytes 4718592 | tf_op jit(solution)/shard_map/all_to_all | solution.py:313
  316.4 78.6 %collective-permute-start.4 = (f32[8,96,384]{2,0,1:T(8,128)}, f32[8,96,384]{2,0,1:T(8,128)}, u32[]{:S(2)}, u32[]{:S(2)}) collective-permute-start(f32[8,96,384]{2,0,1:T(8,128)} %get-tuple-element.29), channel_id=1, source_target_pairs={{0,16},{8,24},{16,0},{24,8},{1,17},{9,25},{17,1},{25,9},{2,18},{10... | collective-permute-start | bytes 3538952 | tf_op jit(solution)/shard_map/ppermute | solution.py:378
  318.0 80.3 %collective-permute-start.3 = (f32[8,96,384]{2,0,1:T(8,128)}, f32[8,96,384]{2,0,1:T(8,128)}, u32[]{:S(2)}, u32[]{:S(2)}) collective-permute-start(f32[8,96,384]{2,0,1:T(8,128)} %get-tuple-element.27), channel_id=1, source_target_pairs={{0,8},{8,16},{16,24},{24,0},{1,9},{9,17},{17,25},{25,1},{2,10},{10... | collective-permute-start | bytes 3538952 | tf_op jit(solution)/shard_map/ppermute | solution.py:378
  323.2 80.7 %slice-start.2 = ((s8[4718592]{0:T(1024)(128)(4,1)}), s8[4194304]{0:T(1024)(128)(4,1)S(1)}, s32[]{:S(2)}) async-start(s8[4718592]{0:T(1024)(128)(4,1)} %bitcast.196), calls=%async_computation.8 | async-start | bytes 8388608
  326.8 77.1 %slice-start.3 = ((s8[4718592]{0:T(1024)(128)(4,1)}), s8[524288]{0:T(1024)(128)(4,1)S(1)}, s32[]{:S(2)}) async-start(s8[4718592]{0:T(1024)(128)(4,1)} %bitcast.196), calls=%async_computation.9 | async-start | bytes 1048576
  433.2 110.5 %all-to-all-start.4 = ((f32[32,288,128]{2,1,0:T(8,128)}), f32[32,288,128]{2,1,0:T(8,128)}, u32[]{:S(2)}, u32[]{:S(2)}) async-start(f32[32,288,128]{2,1,0:T(8,128)} %reshape.159), calls=%async_computation.4 | async-start | bytes 9437184 | tf_op jit(solution)/shard_map/all_to_all | solution.py:313
  437.1 6.7 %copy-start.15 = (f32[4,96,384]{2,1,0:T(8,128)S(1)}, f32[4,96,384]{2,1,0:T(8,128)}, u32[]{:S(2)}) copy-start(f32[4,96,384]{2,1,0:T(8,128)} %constant.250) | copy-start | bytes 1769476
  439.9 50.4 %collective-permute-start.2 = (f32[4,96,384]{2,0,1:T(4,128)S(1)}, f32[4,96,384]{2,0,1:T(4,128)S(1)}, u32[]{:S(2)}, u32[]{:S(2)}) collective-permute-start(f32[4,96,384]{2,0,1:T(4,128)S(1)} %get-tuple-element.32), channel_id=1, source_target_pairs={{0,24},{8,0},{16,8},{24,16},{1,25},{9,1},{17,9},{25,17},{2,26},{10... | collective-permute-start | bytes 1769480 | tf_op jit(solution)/shard_map/ppermute | solution.py:378
  442.5 48.9 %collective-permute-start.1 = (f32[4,96,384]{2,0,1:T(4,128)S(1)}, f32[4,96,384]{2,0,1:T(4,128)S(1)}, u32[]{:S(2)}, u32[]{:S(2)}) collective-permute-start(f32[4,96,384]{2,0,1:T(4,128)S(1)} %get-tuple-element.33), channel_id=1, source_target_pairs={{0,16},{8,24},{16,0},{24,8},{1,17},{9,25},{17,1},{25,9},{2,18},{10... | collective-permute-start | bytes 1769480 | tf_op jit(solution)/shard_map/ppermute | solution.py:378
  443.1 70.1 %collective-permute-start = (f32[4,96,384]{2,0,1:T(4,128)S(1)}, f32[4,96,384]{2,0,1:T(4,128)S(1)}, u32[]{:S(2)}, u32[]{:S(2)}) collective-permute-start(f32[4,96,384]{2,0,1:T(4,128)S(1)} %get-tuple-element.31), channel_id=1, source_target_pairs={{0,8},{8,16},{16,24},{24,0},{1,9},{9,17},{17,25},{25,1},{2,10},{10... | collective-permute-start | bytes 1769480 | tf_op jit(solution)/shard_map/ppermute | solution.py:378
  543.7 58.6 %all-to-all-start.5 = ((f32[32,144,128]{2,1,0:T(8,128)}), f32[32,144,128]{2,1,0:T(8,128)S(1)}, u32[]{:S(2)}, u32[]{:S(2)}) async-start(f32[32,144,128]{2,1,0:T(8,128)} %reshape.158), calls=%async_computation.5 | async-start | bytes 4718592 | tf_op jit(solution)/shard_map/all_to_all | solution.py:313
  583.7 18.5 %copy-start.6 = (bf16[128,384]{1,0:T(8,128)(2,1)S(1)}, bf16[128,384]{1,0:T(8,128)(2,1)}, u32[]{:S(2)}) copy-start(bf16[128,384]{1,0:T(8,128)(2,1)} %constant.239.clone.high) | copy-start | bytes 294916
  583.7 18.5 %copy-start.8 = (bf16[128,384]{1,0:T(8,128)(2,1)S(1)}, bf16[128,384]{1,0:T(8,128)(2,1)}, u32[]{:S(2)}) copy-start(bf16[128,384]{1,0:T(8,128)(2,1)} %constant.240.clone.low) | copy-start | bytes 294916
  (12 other events, 37.9 us)

commit v4 on v3

--- a/solution.py
+++ b/solution.py
@@ -1,3 +1,5 @@
+import functools
+
 import jax
 import jax.numpy as jnp
 import numpy as np
@@ -221,20 +223,25 @@
     )(jnp.asarray(high), jnp.asarray(low), last, photon, density)
 
 
-def gather_kernel(mine, everyone, send_sems, receive_sems):
+def gather_kernel(inner, mine, everyone, send_sems, receive_sems):
     count = everyone.shape[0]
-    me = lax.axis_index("py")
+    me = lax.axis_index("ph") * inner + lax.axis_index("pl")
+
+    def peer(shift):
+        other = lax.rem(me + shift, count)
+        return {"ph": lax.div(other, inner), "pl": lax.rem(other, inner)}
+
     barrier = pltpu.get_barrier_semaphore()
     for shift in range(1, count):
         pl.semaphore_signal(
-            barrier, inc=1, device_id={"py": lax.rem(me + shift, count)},
+            barrier, inc=1, device_id=peer(shift),
             device_id_type=pl.DeviceIdType.MESH,
         )
     pl.semaphore_wait(barrier, count - 1)
     copies = [
         pltpu.make_async_remote_copy(
             mine, everyone.at[me], send_sems.at[shift], receive_sems.at[shift],
-            device_id={"py": lax.rem(me + shift, count)},
+            device_id=peer(shift),
             device_id_type=pl.DeviceIdType.MESH,
         )
         for shift in range(1, count)
@@ -246,10 +253,10 @@
         copy.wait()
 
 
-def gather(mine, count):
+def gather(mine, count, inner):
     vmem = pl.BlockSpec(memory_space=pltpu.VMEM)
     return pl.pallas_call(
-        gather_kernel,
+        functools.partial(gather_kernel, inner),
         out_shape=jax.ShapeDtypeStruct((count,) + mine.shape, mine.dtype),
         in_specs=[vmem],
         out_specs=vmem,
@@ -263,9 +270,10 @@
     rows_x, rows_y, grid = density.shape
     slots = photons.shape[1]
     count_x = lax.axis_size("px")
-    count_y = lax.axis_size("py")
-    place_x = lax.axis_index("px")
-    place_y = lax.axis_index("py")
+    count_h, count_l = lax.axis_size("ph"), lax.axis_size("pl")
+    count_y = count_h * count_l
+    place_x, place_h, place_l = (lax.axis_index(name) for name in ("px", "ph", "pl"))
+    place_y = place_h * count_l + place_l
     devices_all = count_x * count_y
     planes = grid // devices_all
     area = rows_x * rows_y
@@ -277,12 +285,14 @@
     first = max(1, planes * 2 // 3)
     assert first < planes
     parts = [(0, first), (first, planes)]
+    shared = np.arange(grid).reshape(count_x, count_h, count_l, planes)[..., first:]
+    shared = shared.transpose(0, 2, 1, 3).reshape(count_x, count_l, -1)
     by_plane = table_np.reshape(grid, devices_all, planes)
     tables = [by_plane[:, :, a:b].reshape(grid, devices_all * (b - a)) for a, b in parts]
 
     pair = LANES // 2
     width = pair // count_x
-    assert planes <= width and rows_x % 2 == 0
+    assert rows_x % 2 == 0
     assert 2 * grid <= 1 << TAB_BITS and rows_x * grid * grid < 1 << 24
     half_x = rows_x // 2
     rows = grid * half_x
@@ -295,7 +305,7 @@
     row = (cell_x // 2) * grid + cell_y
     key = jnp.where(live, row * (2 * grid) + (cell_x % 2) * grid + cell_z, 0)
     sent = jnp.concatenate([weights, key.astype(jnp.float32)])
-    slab = gather(sent, count_y).reshape(count_y, 2, -1, slots)
+    slab = gather(sent, count_y, count_l).reshape(count_y, 2, -1, slots)
     slab = [slab[:, kind].reshape(-1, slots) for kind in range(2)]
     slab, density = lax.optimization_barrier((slab, density))
 
@@ -306,12 +316,12 @@
 
     received = []
 
-    def exchange(blocks_out):
-        blocks_out = blocks_out.reshape(devices_all, -1, LANES)
+    def exchange(blocks_out, among=("px", "ph", "pl")):
+        blocks_out = blocks_out.reshape(lax.axis_size(among), -1, LANES)
         if received:
             blocks_out, _ = lax.optimization_barrier((blocks_out, received[-1]))
         got = lax.all_to_all(
-            blocks_out, ("px", "py"), split_axis=0, concat_axis=0, tiled=True
+            blocks_out, among, split_axis=0, concat_axis=0, tiled=True
         )
         received.append(got)
         return got
@@ -321,34 +331,51 @@
 
     freq = signed(jnp.arange(grid, dtype=jnp.int32))
     freq_z = signed(
-        lax.axis_index(("px", "py")) * planes + jnp.arange(planes, dtype=jnp.int32)
-    )
-    windows = [
-        lax.optimization_barrier(
-            top_hat(freq_z[a:b, None, None], freq[None, :, None], freq[None, None, :], grid)
+        (place_x * count_y + place_y) * planes + jnp.arange(planes, dtype=jnp.int32)
+    )
+    shared_z = signed(jnp.asarray(shared, dtype=jnp.int32)[place_x, place_l])
+
+    def window_of(freq_z):
+        return lax.optimization_barrier(
+            top_hat(freq_z[:, None, None], freq[None, :, None], freq[None, None, :], grid)
         )
-        for a, b in parts
-    ]
+
+    rest = window_of(jnp.concatenate([freq_z[first:], shared_z]))
+    windows = [window_of(freq_z[:first]), rest[: planes - first]]
+    shared_window = rest[planes - first :]
 
     all_keys = slab[1].astype(jnp.int32)
     all_keys = all_keys // (2 * grid) * (1 << TAB_BITS) + all_keys % (2 * grid)
     all_counts = jnp.max(jnp.where(slab[0] != 0.0, slot_index + 1, 0), axis=1)
-    own = lax.dynamic_index_in_dim(
-        table.reshape(grid, count_x, count_y, planes), place_y, 2, keepdims=False
-    )
-    own = jnp.pad(own, ((0, 0), (0, 0), (0, width - planes))).reshape(grid, pair)
+    alone = np.arange(grid).reshape(count_x, count_y, planes)[..., :first]
+    columns = np.concatenate(
+        [
+            alone.transpose(1, 0, 2),
+            np.tile(shared.transpose(1, 0, 2), (count_h, 1, 1)),
+        ],
+        axis=2,
+    )
+    used = columns.shape[2]
+    assert used <= width
+    own = np.zeros((count_y, grid, count_x, width), np.float32)
+    own[..., :used] = table_np[:, columns].transpose(1, 0, 2, 3)
+    own = jnp.asarray(own.reshape(count_y, grid, pair))[place_y]
     waves = jnp.concatenate(
         [jnp.pad(own, ((0, 0), (0, pair))), jnp.pad(own, ((0, 0), (pair, 0)))]
     )
     painted = paint(all_keys, slab[0], all_counts, waves, rows)
     for spec in specs[1:]:
-        spec, painted, windows[0] = lax.optimization_barrier((spec, painted, windows[0]))
+        spec, painted = lax.optimization_barrier((spec, painted))
         density_got.append(exchange(spec))
 
-    def outward(full):
-        half = product("kmn,qlm->qkln", full, table_y)
+    half_y = lax.dynamic_index_in_dim(
+        table_y.reshape(count_h, count_l, rows_y, grid), place_h, 0, keepdims=False
+    )
+
+    def outward(full, sums_y=table_y, among=("px", "ph", "pl")):
+        half = product("kmn,qlm->qkln", full, sums_y)
         back = product("qkln,ixn->iqklx", half, table_x)
-        return exchange(back)
+        return exchange(back, among)
 
     def inward(got):
         got = got.reshape(count_x, count_y, -1, rows_y, rows_x)
@@ -356,7 +383,7 @@
         return product("qkln,qlm->kmn", half, table_y)
 
     lines = product("ayc,ym->acm", painted.reshape(half_x, grid, LANES), table)
-    lines = lines.reshape(rows_x, count_x, width, grid)[:, :, :planes]
+    lines = lines.reshape(rows_x, count_x, width, grid)[:, :, :used]
     lines = lines.transpose(1, 2, 0, 3)
     rows_of = [
         lax.dynamic_index_in_dim(table_x, (place_x - shift) % count_x, 0, keepdims=False)
@@ -369,7 +396,7 @@
             )[0]
             for shift in range(count_x)
         ]
-        for a, b in parts
+        for a, b in ((0, first), (first, used))
     ]
 
     def around(block, shift):
@@ -390,9 +417,11 @@
         return total
 
     density_back = [outward(inward(got) * win) for got, win in zip(density_got, windows)]
-    photon_back = [
-        outward(crosswise(blocks) * win) for blocks, win in zip(photon_parts, windows)
-    ]
+    across = crosswise(photon_parts[0])
+    photon_first = outward(across * windows[0])
+    photon_last = outward(
+        crosswise(photon_parts[1]) * shared_window, half_y, ("px", "pl")
+    )
 
     def backward(got):
         total = None
@@ -402,21 +431,19 @@
         return total
 
     density_smooth = backward(density_back)
-    photon_smooth = backward(photon_back[:-1])
+    photon_smooth = backward([photon_first])
     return finish(
-        photon_back[-1], photon_smooth, density_smooth, tables[-1], rows_x, rows_y
+        photon_last, photon_smooth, density_smooth, table_np[:, shared.reshape(-1)], rows_x, rows_y
     )
 
 
 def solution(mesh):
-    placed = (
-        P(("px", "py"), None),
-        P(("px", "py"), None),
-        P(("px", "py")),
-        P(("px", "py"), None),
-        P("px", "py", None),
-    )
+    devices = mesh.devices
+    count_x, count_y = devices.shape
+    inner = jax.sharding.Mesh(devices.reshape(count_x, 2, count_y // 2), ("px", "ph", "pl"))
+    every, split = ("px", "ph", "pl"), ("ph", "pl")
+    placed = (P(every, None), P(every, None), P(every), P(every, None), P("px", split, None))
 
     return jax.shard_map(
-        on_device, mesh=mesh, in_specs=placed, out_specs=P("px", "py", None), check_vma=False
-    )
+        on_device, mesh=inner, in_specs=placed, out_specs=P("px", split, None), check_vma=False
+    )

time: 623 us -> 641 us (1.029)
  matrix products: 125 us -> 143 us
  other arithmetic: 18.1 us -> 29.4 us
  waiting for transfers between devices: 226 us -> 219 us
    all_to_all x6, waiting for transfers between devices: 92.4 us -> 54.7 us  [exchange(): lax.all_to_all(blocks_out, among, split_axis=0, concat_axis=0, tiled=True)]
    ppermute x6, waiting for transfers between devices: 134 us -> 164 us  [around(): lax.ppermute(block, 'px', [(i, (i + shift) % count_x) for i in range(coun...]
    dot_general x24, matrix products: 125 us -> 143 us  [product(): return jnp.einsum(form, left, right, precision=lax.Precision.HIGH)]
    select_n x2, other arithmetic: 14.7 us -> 25.3 us  [top_hat(): return jnp.where(radial > 0, value, 1.0)]
    unnamed x48 -> x50, local copies, waits for them, and re-layouts: 19.1 us -> 16.8 us
    reshape x5 -> x4, local copies, waits for them, and re-layouts: 23.5 us -> 23.7 us  [exchange(): blocks_out = blocks_out.reshape(lax.axis_size(among), -1, LANES)]
  transfers between devices with their start and end apart: 12 -> 12, of which waited for: 8 -> 6; matrix products, arithmetic and copies ran while one was open for 35% -> 38% of each run, Pallas kernels for 14% -> 14%
where the time goes in v4:
time: 641 us; the launch traced here: 633 us
  waiting for transfers between devices  219 us (34%)
  matrix products  143 us (22%)
  Pallas kernels  114 us (18%)
  local copies, waits for them, and re-layouts  89.9 us (14%)
  starting transfers between devices  36.8 us (6%)
  other arithmetic  29.4 us (5%)
    ppermute x6, waiting for transfers between devices, around(): lax.ppermute(block, 'px', [(i, (i + shift) % count_x) for i in range(coun...  164 us
    dot_general x24, matrix products, product(): return jnp.einsum(form, left, right, precision=lax.Precision.HIGH)  143 us
    pallas_call x1, Pallas kernels, paint(): pl.pallas_call(paint_kernel, out_shape=jax.ShapeDtypeStruct((rows, LANES)...  79.9 us
    all_to_all x6, waiting for transfers between devices, exchange(): lax.all_to_all(blocks_out, among, split_axis=0, concat_axis=0, tiled=True)  54.7 us
    all_to_all x6, starting transfers between devices, exchange(): lax.all_to_all(blocks_out, among, split_axis=0, concat_axis=0, tiled=True)  27.3 us
    select_n x2, other arithmetic, top_hat(): return jnp.where(radial > 0, value, 1.0)  25.3 us
    reshape x4, local copies, waits for them, and re-layouts, exchange(): blocks_out = blocks_out.reshape(lax.axis_size(among), -1, LANES)  23.7 us
    unnamed x50, local copies, waits for them, and re-layouts  16.8 us
  transfers between devices with their start and end apart: 12, of which 6 were waited for; matrix products, arithmetic and copies ran while one was open for 38% of the time, Pallas kernels for 14%

profile of v4, /device:TPU:0, one launch (start us, length us, event | category | flops | bytes accessed | tf_op | source)
XLA Modules:
  0.0 632.9 jit_solution(2566667293026198077)
XLA Ops:
  2.9 11.7 %gather.1 = f32[8,64,128]{2,1,0:T(8,128)} custom-call(f32[64,128]{1,0:T(8,128)} %pad_maximum_fusion.mine), custom_call_target="tpu_custom_call" | custom-call | tf_op jit(solution)/shard_map/gather/pallas_call | solution.py:258
  28.6 6.5 %all-to-all-start = ((f32[32,288,128]{2,1,0:T(8,128)}), f32[32,288,128]{2,1,0:T(8,128)}, u32[]{:S(2)}, u32[]{:S(2)}) async-start(f32[32,288,128]{2,1,0:T(8,128)} %bitcast.198), calls=%async_computation | async-start | bytes 9437184 | tf_op jit(solution)/shard_map/all_to_all | solution.py:323
  39.3 6.7 %spread.2 = f32[4608,128]{1,0:T(8,128)} custom-call(bf16[128,384]{1,0:T(8,128)(2,1)S(1)} %copy-done.9, bf16[128,384]{1,0:T(8,128)(2,1)S(1)} %copy-done.10, f32[96,48,384]{2,1,0:T(8,128)S(1)} %copy-done.2), custom_call_target="tpu_custom_call" | custom-call | flops 1358954496 | bytes 9437184 | tf_op jit(solution)/shard_map/spread/pallas_call | solution.py:153
  46.2 79.9 %paint.1 = f32[18432,128]{1,0:T(8,128)S(1)} custom-call(s32[256,128]{1,0:T(8,128)S(1)} %get-tuple-element.35.key, f32[256,128]{1,0:T(8,128)S(1)} %bitcast.202, s32[256]{0:T(256)S(1)} %get-tuple-element.36.count, f32[768,128]{1,0:T(8,128)S(1)} %select_maximum_fusion.waves), custom_call_target="tpu_custom_call" | custom-call | flops 80000000000 | bytes 9437184 | tf_op jit(solution)/shard_map/paint/pallas_call | solution.py:92
  129.8 11.6 %all-to-all-done = f32[32,288,128]{2,1,0:T(8,128)} async-done(((f32[32,288,128]{2,1,0:T(8,128)}), f32[32,288,128]{2,1,0:T(8,128)}, u32[]{:S(2)}, u32[]{:S(2)}) %all-to-all-start) | async-done | bytes 4718624 | tf_op jit(solution)/shard_map/all_to_all | solution.py:323
  145.0 10.3 %compare_select_fusion.2 = f32[8,384,384]{2,1,0:T(8,128)} fusion(f32[384]{0:T(512)S(1)} %fusion.156, f32[8,384]{1,0:T(8,128)S(1)} %broadcast_add_fusion.1), kind=kLoop, calls=%fused_computation.42 | loop fusion | flops 58982400 | bytes 4732416 | tf_op jit(solution)/shard_map/jit(_where)/select_n | solution.py:55
  155.2 7.2 %reshape.170 = f32[4,8,8,48,96]{4,3,2,1,0:T(8,128)} reshape(f32[32,288,128]{2,1,0:T(8,128)} %all-to-all-done) | data formatting | bytes 9437184 | tf_op jit(solution)/shard_map/reshape | solution.py:381
  162.4 8.1 %fusion.20 = f32[8,8,48,384,1]{3,2,0,1,4:T(8,128)S(1)} fusion(f32[4,96,384,1,1]{2,1,3,4,0:T(8,128)S(1)} %copy-done.14, f32[4,8,8,48,96]{4,3,2,1,0:T(8,128)} %reshape.170), kind=kOutput, calls=%fused_computation.40 | convolution fusion | flops 2717908992 | bytes 10027008 | tf_op jit(solution)/shard_map/iqklx,ixn->qkln/dot_general | solution.py:19
  188.3 7.9 %reshape.171 = f32[32,288,128]{2,1,0:T(8,128)} reshape(f32[4,8,8,48,96]{4,3,2,1,0:T(8,128)} %copy.26) | data formatting | bytes 9437184 | tf_op jit(solution)/shard_map/reshape | solution.py:320
  204.1 9.6 %copy.22 = f32[48,128,384]{2,1,0:T(8,128)} copy(f32[48,128,384]{1,2,0:T(8,128)} %bitcast.200) | data formatting | bytes 18874368 | tf_op jit(solution)/shard_map/ayc,ym->acm/dot_general | solution.py:19
  213.8 11.9 %fusion.161 = f32[96,4,16,384]{3,2,1,0:T(8,128)S(1)} fusion(f32[96,4,16,384]{3,2,1,0:T(8,128)} %bitcast.207, f32[384,384,1,1]{1,0,3,2:T(8,128)S(1)} %copy-done.16), kind=kOutput, calls=%fused_computation.228 | convolution fusion | flops 5435817984 | bytes 19464192 | tf_op jit(solution)/shard_map/ayc,ym->acm/dot_general | solution.py:19
  232.4 15.1 %compare_select_fusion = f32[12,384,384]{2,1,0:T(8,128)} fusion(f32[384]{0:T(512)S(1)} %fusion.156, f32[12,384]{1,0:T(8,128)S(1)} %broadcast_add_fusion), kind=kLoop, calls=%fused_computation.3 | loop fusion | flops 88473600 | bytes 7097856 | tf_op jit(solution)/shard_map/jit(_where)/select_n | solution.py:55
  271.8 38.9 %all-to-all-done.2 = f32[32,288,128]{2,1,0:T(8,128)} async-done(((f32[32,288,128]{2,1,0:T(8,128)}), f32[32,288,128]{2,1,0:T(8,128)}, u32[]{:S(2)}, u32[]{:S(2)}) %all-to-all-start.2) | async-done | bytes 4718624 | tf_op jit(solution)/shard_map/all_to_all | solution.py:323
  324.4 68.4 %collective-permute-done.4 = f32[8,96,384]{2,0,1:T(8,128)} collective-permute-done((f32[8,96,384]{2,0,1:T(8,128)}, f32[8,96,384]{2,0,1:T(8,128)}, u32[]{:S(2)}, u32[]{:S(2)}) %collective-permute-start.4) | collective-permute-done | bytes 1179680 | tf_op jit(solution)/shard_map/ppermute | solution.py:405
  401.7 10.5 %fusion.52 = f32[8,384,8,48]{1,3,0,2:T(8,128)} fusion(f32[8,48,384,1]{2,1,3,0:T(8,128)S(1)} %copy-done.11, f32[8,384,384]{2,1,0:T(8,128)S(1)} %bitcast.206, f32[8,384,384]{2,1,0:T(8,128)S(1)} %fusion.89, f32[8,384,384]{2,1,0:T(8,128)S(1)} %fusion.91, f32[8,384,384]{2,1,0:T(8,128)S(1)} %fusion.95, f32[8,384,384]{2,1,0:T(8,128)} %fusion.93), kind=kOutput, calls=%fused_computation.81 | convolution fusion | flops 2722627584 | bytes 28901376 | tf_op jit(solution)/shard_map/kmn,qlm->qkln/dot_general | solution.py:19
  412.2 7.3 %fusion.66 = f32[4,8,8,48,96]{4,3,0,2,1:T(8,128)S(1)} fusion(f32[4,96,384,1,1]{2,1,0,4,3:T(8,128)S(1)} %copy-done.12, f32[8,384,8,48]{1,3,0,2:T(8,128)} %fusion.52), kind=kOutput, calls=%fused_computation.99 | convolution fusion | flops 2717908992 | bytes 10027008 | tf_op jit(solution)/shard_map/qkln,ixn->iqklx/dot_general | solution.py:19
  423.0 7.9 %reshape.165 = f32[32,288,128]{2,1,0:T(8,128)} reshape(f32[4,8,8,48,96]{4,3,2,1,0:T(8,128)} %copy.24) | data formatting | bytes 9437184 | tf_op jit(solution)/shard_map/reshape | solution.py:320
  440.8 68.6 %collective-permute-done.2 = f32[8,96,384]{2,0,1:T(8,128)} collective-permute-done((f32[8,96,384]{2,0,1:T(8,128)}, f32[8,96,384]{2,0,1:T(8,128)}, u32[]{:S(2)}, u32[]{:S(2)}) %collective-permute-start.2) | collective-permute-done | bytes 1179680 | tf_op jit(solution)/shard_map/ppermute | solution.py:405
  516.5 27.4 %collective-permute-done = f32[8,96,384]{2,0,1:T(8,128)} collective-permute-done((f32[8,96,384]{2,0,1:T(8,128)}, f32[8,96,384]{2,0,1:T(8,128)}, u32[]{:S(2)}, u32[]{:S(2)}) %collective-permute-start) | collective-permute-done | bytes 1179680 | tf_op jit(solution)/shard_map/ppermute | solution.py:405
  549.4 6.6 %fusion.41 = f32[4,48,8,384]{3,1,2,0:T(8,128)} fusion(f32[12,384,384]{2,1,0:T(8,128)S(1)} %bitcast.209, f32[8,384,384]{2,1,0:T(8,128)S(1)} %fusion.97, f32[8,384,384]{2,1,0:T(8,128)S(1)} %fusion.99, f32[8,384,384]{2,1,0:T(8,128)S(1)} %fusion.103, f32[8,384,384]{2,1,0:T(8,128)} %fusion.101, f32[2,4,48,384]{3,2,1,0:T(8,128)S(1)} %copy-done.18, s32[]{:T(128)S(6)} %select_n.197), kind=kOutput, calls=%fused_computation.71 | convolution fusion | flops 1363673088 | bytes 26247172 | tf_op jit(solution)/shard_map/kmn,qlm->qkln/dot_general | solution.py:19
  575.4 12.8 %fusion.163 = f32[4608,384]{1,0:T(8,128)} fusion(f32[256,4608]{1,0:T(8,128)} %reshape.174, f32[384,256]{1,0:T(8,128)S(1)} %copy-done.15), kind=kOutput, calls=%fused_computation.230 | convolution fusion | flops 2717908992 | bytes 12189696 | tf_op jit(solution)/shard_map/ka,zk->az/dot_general | solution.py:19
  591.2 10.5 %convolution_add_fusion.density = f32[4608,384]{1,0:T(8,128)} fusion(f32[4608,384]{1,0:T(8,128)} %fusion.163, f32[128,4608]{1,0:T(8,128)} %reshape.175, f32[384,128]{1,0:T(8,128)S(1)} %copy-done.17), kind=kOutput, calls=%fused_computation.12 | convolution fusion | flops 1360723968 | bytes 16711680 | tf_op jit(solution)/shard_map/ka,zk->az/dot_general | solution.py:19
  607.2 12.8 %fusion.162.photon = f32[4608,384]{1,0:T(8,128)} fusion(f32[256,4608]{1,0:T(8,128)} %reshape.173, f32[384,256]{1,0:T(8,128)S(1)} %copy-done.15), kind=kOutput, calls=%fused_computation.229 | convolution fusion | flops 2717908992 | bytes 12189696 | tf_op jit(solution)/shard_map/ka,zk->az/dot_general | solution.py:19
  623.0 9.4 %finish.1 = f32[96,48,384]{2,1,0:T(8,128)} custom-call(bf16[128,384]{1,0:T(8,128)(2,1)S(1)} %copy-done.7, bf16[128,384]{1,0:T(8,128)(2,1)S(1)} %copy-done.8, f32[4608,128]{1,0:T(8,128)S(1)} %bitcast.199, f32[4608,384]{1,0:T(8,128)S(1)} %copy-done, f32[4608,384]{1,0:T(8,128)} %convolution_add_fusion.density), custom_call_target="tpu_custom_call" | custom-call | flops 1358954496 | bytes 23592960 | tf_op jit(solution)/shard_map/finish/pallas_call | solution.py:203
  (116 shorter events, 164.3 us)
Async XLA Ops:
  28.6 112.7 %all-to-all-start = ((f32[32,288,128]{2,1,0:T(8,128)}), f32[32,288,128]{2,1,0:T(8,128)}, u32[]{:S(2)}, u32[]{:S(2)}) async-start(f32[32,288,128]{2,1,0:T(8,128)} %bitcast.198), calls=%async_computation | async-start | bytes 9437184 | tf_op jit(solution)/shard_map/all_to_all | solution.py:323
  141.4 59.1 %all-to-all-start.1 = ((f32[32,144,128]{2,1,0:T(8,128)}), f32[32,144,128]{2,1,0:T(8,128)}, u32[]{:S(2)}, u32[]{:S(2)}) async-start(f32[32,144,128]{2,1,0:T(8,128)} %bitcast.53), calls=%async_computation.1 | async-start | bytes 4718592 | tf_op jit(solution)/shard_map/all_to_all | solution.py:323
  155.2 19.5 %slice-start = ((s8[4718592]{0:T(1024)(128)(4,1)}), s8[524288]{0:T(1024)(128)(4,1)S(1)}, s32[]{:S(2)}) async-start(s8[4718592]{0:T(1024)(128)(4,1)} %bitcast.203), calls=%async_computation.6 | async-start | bytes 1048576
  162.4 8.2 %copy-start.11 = (f32[8,48,384,1]{2,1,3,0:T(8,128)S(1)}, f32[8,48,384,1]{2,1,3,0:T(8,128)}, u32[]{:S(2)}) copy-start(f32[8,48,384,1]{2,1,3,0:T(8,128)} %constant.271) | copy-start | bytes 1769476
  162.4 12.3 %slice-start.1 = ((s8[4718592]{0:T(1024)(128)(4,1)}), s8[4194304]{0:T(1024)(128)(4,1)S(1)}, s32[]{:S(2)}) async-start(s8[4718592]{0:T(1024)(128)(4,1)} %bitcast.203), calls=%async_computation.7 | async-start | bytes 8388608
  200.5 110.2 %all-to-all-start.2 = ((f32[32,288,128]{2,1,0:T(8,128)}), f32[32,288,128]{2,1,0:T(8,128)}, u32[]{:S(2)}, u32[]{:S(2)}) async-start(f32[32,288,128]{2,1,0:T(8,128)} %reshape.171), calls=%async_computation.2 | async-start | bytes 9437184 | tf_op jit(solution)/shard_map/all_to_all | solution.py:323
  204.1 9.7 %copy-start.16 = (f32[384,384,1,1]{1,0,3,2:T(8,128)S(1)}, f32[384,384,1,1]{1,0,3,2:T(8,128)}, u32[]{:S(2)}) copy-start(f32[384,384,1,1]{1,0,3,2:T(8,128)} %constant.269) | copy-start | bytes 1769476
  229.0 91.8 %collective-permute-start.5 = (f32[8,96,384]{2,0,1:T(8,128)}, f32[8,96,384]{2,0,1:T(8,128)}, u32[]{:S(2)}, u32[]{:S(2)}) collective-permute-start(f32[8,96,384]{2,0,1:T(8,128)} %get-tuple-element.26), channel_id=1, source_target_pairs={{0,24},{8,0},{16,8},{24,16},{1,25},{9,1},{17,9},{25,17},{2,26},{10... | collective-permute-start | bytes 3538952 | tf_op jit(solution)/shard_map/ppermute | solution.py:405
  266.8 50.5 %copy-start.13 = (f32[4,96,384]{2,1,0:T(8,128)S(1)}, f32[4,96,384]{2,1,0:T(8,128)}, u32[]{:S(2)}) copy-start(f32[4,96,384]{2,1,0:T(8,128)} %constant.267) | copy-start | bytes 1769476
  310.7 120.2 %all-to-all-start.3 = ((f32[32,144,128]{2,1,0:T(8,128)}), f32[32,144,128]{2,1,0:T(8,128)}, u32[]{:S(2)}, u32[]{:S(2)}) async-start(f32[32,144,128]{2,1,0:T(8,128)} %reshape.169), calls=%async_computation.3 | async-start | bytes 4718592 | tf_op jit(solution)/shard_map/all_to_all | solution.py:323
  314.2 78.6 %collective-permute-start.4 = (f32[8,96,384]{2,0,1:T(8,128)}, f32[8,96,384]{2,0,1:T(8,128)}, u32[]{:S(2)}, u32[]{:S(2)}) collective-permute-start(f32[8,96,384]{2,0,1:T(8,128)} %get-tuple-element.27), channel_id=1, source_target_pairs={{0,16},{8,24},{16,0},{24,8},{1,17},{9,25},{17,1},{25,9},{2,18},{10... | collective-permute-start | bytes 3538952 | tf_op jit(solution)/shard_map/ppermute | solution.py:405
  315.9 80.3 %collective-permute-start.3 = (f32[8,96,384]{2,0,1:T(8,128)}, f32[8,96,384]{2,0,1:T(8,128)}, u32[]{:S(2)}, u32[]{:S(2)}) collective-permute-start(f32[8,96,384]{2,0,1:T(8,128)} %get-tuple-element.25), channel_id=1, source_target_pairs={{0,8},{8,16},{16,24},{24,0},{1,9},{9,17},{17,25},{25,1},{2,10},{10... | collective-permute-start | bytes 3538952 | tf_op jit(solution)/shard_map/ppermute | solution.py:405
  320.8 80.9 %slice-start.2 = ((s8[4718592]{0:T(1024)(128)(4,1)}), s8[4194304]{0:T(1024)(128)(4,1)S(1)}, s32[]{:S(2)}) async-start(s8[4718592]{0:T(1024)(128)(4,1)} %bitcast.205), calls=%async_computation.8 | async-start | bytes 8388608
  324.4 77.3 %slice-start.3 = ((s8[4718592]{0:T(1024)(128)(4,1)}), s8[524288]{0:T(1024)(128)(4,1)S(1)}, s32[]{:S(2)}) async-start(s8[4718592]{0:T(1024)(128)(4,1)} %bitcast.205), calls=%async_computation.9 | async-start | bytes 1048576
  430.9 133.0 %all-to-all-start.4 = ((f32[32,288,128]{2,1,0:T(8,128)}), f32[32,288,128]{2,1,0:T(8,128)}, u32[]{:S(2)}, u32[]{:S(2)}) async-start(f32[32,288,128]{2,1,0:T(8,128)} %reshape.165), calls=%async_computation.4 | async-start | bytes 9437184 | tf_op jit(solution)/shard_map/all_to_all | solution.py:323
  434.8 74.6 %collective-permute-start.2 = (f32[8,96,384]{2,0,1:T(8,128)}, f32[8,96,384]{2,0,1:T(8,128)}, u32[]{:S(2)}, u32[]{:S(2)}) collective-permute-start(f32[8,96,384]{2,0,1:T(8,128)} %get-tuple-element.29), channel_id=1, source_target_pairs={{0,24},{8,0},{16,8},{24,16},{1,25},{9,1},{17,9},{25,17},{2,26},{10... | collective-permute-start | bytes 3538952 | tf_op jit(solution)/shard_map/ppermute | solution.py:405
  437.5 75.5 %collective-permute-start.1 = (f32[8,96,384]{2,0,1:T(8,128)}, f32[8,96,384]{2,0,1:T(8,128)}, u32[]{:S(2)}, u32[]{:S(2)}) collective-permute-start(f32[8,96,384]{2,0,1:T(8,128)} %get-tuple-element.30), channel_id=1, source_target_pairs={{0,16},{8,24},{16,0},{24,8},{1,17},{9,25},{17,1},{25,9},{2,18},{10... | collective-permute-start | bytes 3538952 | tf_op jit(solution)/shard_map/ppermute | solution.py:405
  438.1 105.9 %collective-permute-start = (f32[8,96,384]{2,0,1:T(8,128)}, f32[8,96,384]{2,0,1:T(8,128)}, u32[]{:S(2)}, u32[]{:S(2)}) collective-permute-start(f32[8,96,384]{2,0,1:T(8,128)} %get-tuple-element.31), channel_id=1, source_target_pairs={{0,8},{8,16},{16,24},{24,0},{1,9},{9,17},{17,25},{25,1},{2,10},{10... | collective-permute-start | bytes 3538952 | tf_op jit(solution)/shard_map/ppermute | solution.py:405
  509.5 39.9 %slice-start.4 = ((s8[7077888]{0:T(1024)(128)(4,1)}), s8[4194304]{0:T(1024)(128)(4,1)S(1)}, s32[]{:S(2)}) async-start(s8[7077888]{0:T(1024)(128)(4,1)} %bitcast.208), calls=%async_computation.10 | async-start | bytes 8388608
  513.0 36.4 %slice-start.5 = ((s8[7077888]{0:T(1024)(128)(4,1)}), s8[2883584]{0:T(1024)(128)(4,1)S(1)}, s32[]{:S(2)}) async-start(s8[7077888]{0:T(1024)(128)(4,1)} %bitcast.208), calls=%async_computation.11 | async-start | bytes 5767168
  513.0 36.4 %copy-start.18 = (f32[2,4,48,384]{3,2,1,0:T(8,128)S(1)}, f32[2,4,48,384]{3,2,1,0:T(8,128)}, u32[]{:S(2)}) copy-start(f32[2,4,48,384]{3,2,1,0:T(8,128)} %constant.266) | copy-start | bytes 1769476
  563.9 56.1 %all-to-all-start.5 = ((f32[16,288,128]{2,1,0:T(8,128)}), f32[16,288,128]{2,1,0:T(8,128)S(1)}, u32[]{:S(2)}, u32[]{:S(2)}) async-start(f32[16,288,128]{2,1,0:T(8,128)} %reshape.163), calls=%async_computation.5 | async-start | bytes 4718592 | tf_op jit(solution)/shard_map/all_to_all | solution.py:323
  607.2 12.8 %copy-start.7 = (bf16[128,384]{1,0:T(8,128)(2,1)S(1)}, bf16[128,384]{1,0:T(8,128)(2,1)}, u32[]{:S(2)}) copy-start(bf16[128,384]{1,0:T(8,128)(2,1)} %constant.260.clone.high) | copy-start | bytes 294916
  607.2 12.8 %copy-start.8 = (bf16[128,384]{1,0:T(8,128)(2,1)S(1)}, bf16[128,384]{1,0:T(8,128)(2,1)}, u32[]{:S(2)}) copy-start(bf16[128,384]{1,0:T(8,128)(2,1)} %constant.261.clone.low) | copy-start | bytes 294916
  (13 other events, 51.9 us)

commit v5 on v4

--- a/solution.py
+++ b/solution.py
@@ -166,7 +166,7 @@
             bytes_accessed=4 * rows_x * rows_y * (grid + count),
             transcendentals=0,
         ),
-        compiler_params=pltpu.CompilerParams(vmem_limit_bytes=40 << 20),
+        compiler_params=pltpu.CompilerParams(vmem_limit_bytes=62 << 20),
         name="spread",
     )(jnp.asarray(high), jnp.asarray(low), density)
 
@@ -218,7 +218,7 @@
             bytes_accessed=4 * rows_x * rows_y * (3 * grid + count),
             transcendentals=0,
         ),
-        compiler_params=pltpu.CompilerParams(vmem_limit_bytes=40 << 20),
+        compiler_params=pltpu.CompilerParams(vmem_limit_bytes=62 << 20),
         name="finish",
     )(jnp.asarray(high), jnp.asarray(low), last, photon, density)
 
@@ -372,10 +372,12 @@
         table_y.reshape(count_h, count_l, rows_y, grid), place_h, 0, keepdims=False
     )
 
-    def outward(full, sums_y=table_y, among=("px", "ph", "pl")):
+    def rows_back(full, sums_y):
         half = product("kmn,qlm->qkln", full, sums_y)
-        back = product("qkln,ixn->iqklx", half, table_x)
-        return exchange(back, among)
+        return product("qkln,ixn->iqklx", half, table_x)
+
+    def outward(full):
+        return exchange(rows_back(full, table_y))
 
     def inward(got):
         got = got.reshape(count_x, count_y, -1, rows_y, rows_x)
@@ -419,9 +421,6 @@
     density_back = [outward(inward(got) * win) for got, win in zip(density_got, windows)]
     across = crosswise(photon_parts[0])
     photon_first = outward(across * windows[0])
-    photon_last = outward(
-        crosswise(photon_parts[1]) * shared_window, half_y, ("px", "pl")
-    )
 
     def backward(got):
         total = None
@@ -431,6 +430,9 @@
         return total
 
     density_smooth = backward(density_back)
+    last = rows_back(crosswise(photon_parts[1]) * shared_window, half_y)
+    last, density_smooth = lax.optimization_barrier((last, density_smooth))
+    photon_last = exchange(last, ("px", "pl"))
     photon_smooth = backward([photon_first])
     return finish(
         photon_last, photon_smooth, density_smooth, table_np[:, shared.reshape(-1)], rows_x, rows_y

time: 641 us -> 654 us (1.020)
  waiting for transfers between devices: 219 us -> 237 us
  local copies, waits for them, and re-layouts: 89.9 us -> 79 us
  Pallas kernels: 114 us -> 122 us
    all_to_all x6, waiting for transfers between devices: 54.7 us -> 72.6 us  [exchange(): lax.all_to_all(blocks_out, among, split_axis=0, concat_axis=0, tiled=True)]
    unnamed x50 -> x44, local copies, waits for them, and re-layouts: 16.8 us -> 6.51 us
  transfers between devices with their start and end apart: 12 -> 12, of which waited for: 6 -> 7; matrix products, arithmetic and copies ran while one was open for 38% -> 37% of each run, Pallas kernels for 14% -> 14%
where the time goes in v5:
time: 654 us; the launch traced here: 646 us
  waiting for transfers between devices  237 us (36%)
  matrix products  142 us (22%)
  Pallas kernels  122 us (19%)
  local copies, waits for them, and re-layouts  79 us (12%)
  starting transfers between devices  35.6 us (5%)
  other arithmetic  29.4 us (4%)
    ppermute x6, waiting for transfers between devices, around(): lax.ppermute(block, 'px', [(i, (i + shift) % count_x) for i in range(coun...  164 us
    dot_general x24, matrix products, product(): return jnp.einsum(form, left, right, precision=lax.Precision.HIGH)  142 us
    pallas_call x1, Pallas kernels, paint(): pl.pallas_call(paint_kernel, out_shape=jax.ShapeDtypeStruct((rows, LANES)...  79.9 us
    all_to_all x6, waiting for transfers between devices, exchange(): lax.all_to_all(blocks_out, among, split_axis=0, concat_axis=0, tiled=True)  72.6 us
    all_to_all x6, starting transfers between devices, exchange(): lax.all_to_all(blocks_out, among, split_axis=0, concat_axis=0, tiled=True)  25.7 us
    select_n x2, other arithmetic, top_hat(): return jnp.where(radial > 0, value, 1.0)  25.3 us
    reshape x4, local copies, waits for them, and re-layouts, exchange(): blocks_out = blocks_out.reshape(lax.axis_size(among), -1, LANES)  23.9 us
    pallas_call x2, Pallas kernels, spread(): pl.pallas_call(spread_kernel, grid=(rows_y // SUBLANES,), out_shape=jax.S...  18.6 us
  transfers between devices with their start and end apart: 12, of which 7 were waited for; matrix products, arithmetic and copies ran while one was open for 37% of the time, Pallas kernels for 14%

profile of v5, /device:TPU:0, one launch (start us, length us, event | category | flops | bytes accessed | tf_op | source)
XLA Modules:
  0.0 645.7 jit_solution(7390229688158953838)
XLA Ops:
  2.9 11.7 %gather.1 = f32[8,64,128]{2,1,0:T(8,128)} custom-call(f32[64,128]{1,0:T(8,128)} %pad_maximum_fusion.mine), custom_call_target="tpu_custom_call" | custom-call | tf_op jit(solution)/shard_map/gather/pallas_call | solution.py:258
  15.5 9.9 %spread.3 = f32[9216,128]{1,0:T(8,128)} custom-call(bf16[256,384]{1,0:T(8,128)(2,1)} %constant.252.clone.high, bf16[256,384]{1,0:T(8,128)(2,1)} %constant.253.clone.low, f32[96,48,384]{2,1,0:T(8,128)} %density.1), custom_call_target="tpu_custom_call" | custom-call | flops 2717908992 | bytes 11796480 | tf_op jit(solution)/shard_map/spread/pallas_call | solution.py:153
  33.1 8.6 %spread.2 = f32[4608,128]{1,0:T(8,128)} custom-call(bf16[128,384]{1,0:T(8,128)(2,1)} %constant.254.clone.high, bf16[128,384]{1,0:T(8,128)(2,1)} %constant.255.clone.low, f32[96,48,384]{2,1,0:T(8,128)} %density.1), custom_call_target="tpu_custom_call" | custom-call | flops 1358954496 | bytes 9437184 | tf_op jit(solution)/shard_map/spread/pallas_call | solution.py:153
  41.9 79.9 %paint.1 = f32[18432,128]{1,0:T(8,128)S(1)} custom-call(s32[256,128]{1,0:T(8,128)S(1)} %get-tuple-element.39.key, f32[256,128]{1,0:T(8,128)S(1)} %bitcast.200, s32[256]{0:T(256)S(1)} %get-tuple-element.40.count, f32[768,128]{1,0:T(8,128)S(1)} %select_maximum_fusion.waves), custom_call_target="tpu_custom_call" | custom-call | flops 80000000000 | bytes 9437184 | tf_op jit(solution)/shard_map/paint/pallas_call | solution.py:92
  125.6 12.6 %all-to-all-done = f32[32,288,128]{2,1,0:T(8,128)} async-done(((f32[32,288,128]{2,1,0:T(8,128)}), f32[32,288,128]{2,1,0:T(8,128)}, u32[]{:S(2)}, u32[]{:S(2)}) %all-to-all-start) | async-done | bytes 4718624 | tf_op jit(solution)/shard_map/all_to_all | solution.py:323
  141.0 10.2 %compare_select_fusion.2 = f32[8,384,384]{1,2,0:T(8,128)} fusion(f32[384]{0:T(512)S(1)} %fusion.156, f32[8,384]{1,0:T(8,128)S(1)} %broadcast_add_fusion.1), kind=kLoop, calls=%fused_computation.42 | loop fusion | flops 58982400 | bytes 4732416 | tf_op jit(solution)/shard_map/jit(_where)/select_n | solution.py:55
  151.2 7.1 %reshape.164 = f32[4,8,8,48,96]{4,3,2,1,0:T(8,128)} reshape(f32[32,288,128]{2,1,0:T(8,128)} %all-to-all-done) | data formatting | bytes 9437184 | tf_op jit(solution)/shard_map/reshape | solution.py:383
  158.3 8.1 %fusion.20 = f32[8,8,48,384,1]{3,2,0,1,4:T(8,128)S(1)} fusion(f32[4,96,384,1,1]{2,1,3,4,0:T(8,128)S(1)} %copy-done.13, f32[4,8,8,48,96]{4,3,2,1,0:T(8,128)} %reshape.164), kind=kOutput, calls=%fused_computation.40 | convolution fusion | flops 2717908992 | bytes 10027008 | tf_op jit(solution)/shard_map/iqklx,ixn->qkln/dot_general | solution.py:19
  185.0 7.9 %reshape.166 = f32[32,288,128]{2,1,0:T(8,128)} reshape(f32[4,8,8,48,96]{4,3,2,1,0:T(8,128)} %copy.23) | data formatting | bytes 9437184 | tf_op jit(solution)/shard_map/reshape | solution.py:320
  201.6 9.6 %copy.22 = f32[48,128,384]{2,1,0:T(8,128)} copy(f32[48,128,384]{1,2,0:T(8,128)} %bitcast.198) | data formatting | bytes 18874368 | tf_op jit(solution)/shard_map/ayc,ym->acm/dot_general | solution.py:19
  211.3 11.9 %fusion.161 = f32[96,4,16,384]{3,2,1,0:T(8,128)S(1)} fusion(f32[96,4,16,384]{3,2,1,0:T(8,128)} %bitcast.205, f32[384,384,1,1]{1,0,3,2:T(8,128)S(1)} %copy-done.15), kind=kOutput, calls=%fused_computation.228 | convolution fusion | flops 5435817984 | bytes 19464192 | tf_op jit(solution)/shard_map/ayc,ym->acm/dot_general | solution.py:19
  230.4 15.1 %compare_select_fusion = f32[12,384,384]{2,1,0:T(8,128)} fusion(f32[384]{0:T(512)S(1)} %fusion.156, f32[12,384]{1,0:T(8,128)S(1)} %broadcast_add_fusion), kind=kLoop, calls=%fused_computation.3 | loop fusion | flops 88473600 | bytes 7097856 | tf_op jit(solution)/shard_map/jit(_where)/select_n | solution.py:55
  264.4 43.7 %all-to-all-done.2 = f32[32,288,128]{2,1,0:T(8,128)} async-done(((f32[32,288,128]{2,1,0:T(8,128)}), f32[32,288,128]{2,1,0:T(8,128)}, u32[]{:S(2)}, u32[]{:S(2)}) %all-to-all-start.2) | async-done | bytes 4718624 | tf_op jit(solution)/shard_map/all_to_all | solution.py:323
  321.1 68.5 %collective-permute-done.4 = f32[8,96,384]{2,0,1:T(8,128)} collective-permute-done((f32[8,96,384]{2,0,1:T(8,128)}, f32[8,96,384]{2,0,1:T(8,128)}, u32[]{:S(2)}, u32[]{:S(2)}) %collective-permute-start.4) | collective-permute-done | bytes 1179680 | tf_op jit(solution)/shard_map/ppermute | solution.py:407
  398.5 11.1 %fusion.50 = f32[8,384,8,48]{1,3,0,2:T(8,128)} fusion(f32[8,48,384,1]{2,1,3,0:T(8,128)S(1)} %copy-done.9, f32[8,384,384]{1,2,0:T(8,128)S(1)} %bitcast.204, f32[8,384,384]{1,2,0:T(8,128)S(1)} %fusion.89, f32[8,384,384]{1,2,0:T(8,128)S(1)} %fusion.91, f32[8,384,384]{1,2,0:T(8,128)S(1)} %fusion.95, f32[8,384,384]{1,2,0:T(8,128)} %fusion.93), kind=kOutput, calls=%fused_computation.79 | convolution fusion | flops 2722627584 | bytes 28901376 | tf_op jit(solution)/shard_map/kmn,qlm->qkln/dot_general | solution.py:19
  409.6 7.3 %fusion.69 = f32[4,8,8,48,96]{4,3,0,2,1:T(8,128)S(1)} fusion(f32[4,96,384,1,1]{2,1,0,4,3:T(8,128)S(1)} %copy-done.3, f32[8,384,8,48]{1,3,0,2:T(8,128)} %fusion.50), kind=kOutput, calls=%fused_computation.100 | convolution fusion | flops 2717908992 | bytes 10027008 | tf_op jit(solution)/shard_map/qkln,ixn->iqklx/dot_general | solution.py:19
  420.5 7.9 %reshape.173 = f32[32,288,128]{2,1,0:T(8,128)} reshape(f32[4,8,8,48,96]{4,3,2,1,0:T(8,128)} %copy.26) | data formatting | bytes 9437184 | tf_op jit(solution)/shard_map/reshape | solution.py:320
  441.3 67.1 %collective-permute-done.2 = f32[8,96,384]{2,0,1:T(8,128)} collective-permute-done((f32[8,96,384]{2,0,1:T(8,128)}, f32[8,96,384]{2,0,1:T(8,128)}, u32[]{:S(2)}, u32[]{:S(2)}) %collective-permute-start.2) | collective-permute-done | bytes 1179680 | tf_op jit(solution)/shard_map/ppermute | solution.py:407
  514.0 28.8 %collective-permute-done = f32[8,96,384]{2,0,1:T(8,128)S(1)} collective-permute-done((f32[8,96,384]{2,0,1:T(8,128)}, f32[8,96,384]{2,0,1:T(8,128)S(1)}, u32[]{:S(2)}, u32[]{:S(2)}) %collective-permute-start) | collective-permute-done | bytes 1179680 | tf_op jit(solution)/shard_map/ppermute | solution.py:407
  563.3 12.8 %fusion.162 = f32[4608,384]{1,0:T(8,128)} fusion(f32[256,4608]{1,0:T(8,128)} %reshape.168, f32[384,256]{1,0:T(8,128)S(1)} %copy-done.14), kind=kOutput, calls=%fused_computation.229 | convolution fusion | flops 2717908992 | bytes 12189696 | tf_op jit(solution)/shard_map/ka,zk->az/dot_general | solution.py:19
  579.0 10.6 %convolution_add_fusion.density = f32[4608,384]{1,0:T(8,128)} fusion(f32[4608,384]{1,0:T(8,128)} %fusion.162, f32[128,4608]{1,0:T(8,128)} %reshape.171, f32[384,128]{1,0:T(8,128)} %constant.259.clone), kind=kOutput, calls=%fused_computation.12 | convolution fusion | flops 1360723968 | bytes 16711680 | tf_op jit(solution)/shard_map/ka,zk->az/dot_general | solution.py:19
  608.0 12.8 %fusion.163.photon = f32[4608,384]{1,0:T(8,128)} fusion(f32[256,4608]{1,0:T(8,128)} %reshape.175, f32[384,256]{1,0:T(8,128)S(1)} %copy-done.14), kind=kOutput, calls=%fused_computation.230 | convolution fusion | flops 2717908992 | bytes 12189696 | tf_op jit(solution)/shard_map/ka,zk->az/dot_general | solution.py:19
  620.8 12.5 %all-to-all-done.5 = f32[16,288,128]{2,1,0:T(8,128)} async-done(((f32[16,288,128]{2,1,0:T(8,128)}), f32[16,288,128]{2,1,0:T(8,128)}, u32[]{:S(2)}, u32[]{:S(2)}) %all-to-all-start.5) | async-done | bytes 2359328 | tf_op jit(solution)/shard_map/all_to_all | solution.py:323
  633.3 12.0 %finish.1 = f32[96,48,384]{2,1,0:T(8,128)} custom-call(bf16[128,384]{1,0:T(8,128)(2,1)} %constant.260.clone.high, bf16[128,384]{1,0:T(8,128)(2,1)} %constant.261.clone.low, f32[4608,128]{1,0:T(8,128)} %bitcast.74.last, f32[4608,384]{1,0:T(8,128)} %fusion.163.photon, f32[4608,384]{1,0:T(8,128)} %convolution_add_fusion.density), custom_call_target="tpu_custom_call" | custom-call | flops 1358954496 | bytes 23592960 | tf_op jit(solution)/shard_map/finish/pallas_call | solution.py:203
  (110 shorter events, 156.9 us)
Async XLA Ops:
  25.5 112.7 %all-to-all-start = ((f32[32,288,128]{2,1,0:T(8,128)}), f32[32,288,128]{2,1,0:T(8,128)}, u32[]{:S(2)}, u32[]{:S(2)}) async-start(f32[32,288,128]{2,1,0:T(8,128)} %bitcast.208), calls=%async_computation | async-start | bytes 9437184 | tf_op jit(solution)/shard_map/all_to_all | solution.py:323
  138.2 58.4 %all-to-all-start.1 = ((f32[32,144,128]{2,1,0:T(8,128)}), f32[32,144,128]{2,1,0:T(8,128)S(1)}, u32[]{:S(2)}, u32[]{:S(2)}) async-start(f32[32,144,128]{2,1,0:T(8,128)} %bitcast.209), calls=%async_computation.1 | async-start | bytes 4718592 | tf_op jit(solution)/shard_map/all_to_all | solution.py:323
  158.3 8.2 %copy-start.7 = (f32[8,48,384,1]{2,1,3,0:T(8,128)S(1)}, f32[8,48,384,1]{2,1,3,0:T(8,128)}, u32[]{:S(2)}) copy-start(f32[8,48,384,1]{2,1,3,0:T(8,128)} %constant.272) | copy-start | bytes 1769476
  158.3 13.3 %slice-start = ((s8[4718592]{0:T(1024)(128)(4,1)}), s8[4194304]{0:T(1024)(128)(4,1)S(1)}, s32[]{:S(2)}) async-start(s8[4718592]{0:T(1024)(128)(4,1)} %bitcast.201), calls=%async_computation.6 | async-start | bytes 8388608
  198.0 110.2 %all-to-all-start.2 = ((f32[32,288,128]{2,1,0:T(8,128)}), f32[32,288,128]{2,1,0:T(8,128)}, u32[]{:S(2)}, u32[]{:S(2)}) async-start(f32[32,288,128]{2,1,0:T(8,128)} %reshape.166), calls=%async_computation.2 | async-start | bytes 9437184 | tf_op jit(solution)/shard_map/all_to_all | solution.py:323
  201.6 9.7 %copy-start.15 = (f32[384,384,1,1]{1,0,3,2:T(8,128)S(1)}, f32[384,384,1,1]{1,0,3,2:T(8,128)}, u32[]{:S(2)}) copy-start(f32[384,384,1,1]{1,0,3,2:T(8,128)} %constant.269) | copy-start | bytes 1769476
  227.0 90.6 %collective-permute-start.5 = (f32[8,96,384]{2,0,1:T(8,128)}, f32[8,96,384]{2,0,1:T(8,128)}, u32[]{:S(2)}, u32[]{:S(2)}) collective-permute-start(f32[8,96,384]{2,0,1:T(8,128)} %get-tuple-element.30), channel_id=1, source_target_pairs={{0,24},{8,0},{16,8},{24,16},{1,25},{9,1},{17,9},{25,17},{2,26},{10... | collective-permute-start | bytes 3538952 | tf_op jit(solution)/shard_map/ppermute | solution.py:407
  264.4 49.7 %copy-start.10 = (f32[4,96,384]{2,1,0:T(8,128)S(1)}, f32[4,96,384]{2,1,0:T(8,128)}, u32[]{:S(2)}) copy-start(f32[4,96,384]{2,1,0:T(8,128)} %constant.267) | copy-start | bytes 1769476
  308.2 120.2 %all-to-all-start.3 = ((f32[32,144,128]{2,1,0:T(8,128)}), f32[32,144,128]{2,1,0:T(8,128)S(1)}, u32[]{:S(2)}, u32[]{:S(2)}) async-start(f32[32,144,128]{2,1,0:T(8,128)} %reshape.170), calls=%async_computation.3 | async-start | bytes 4718592 | tf_op jit(solution)/shard_map/all_to_all | solution.py:323
  310.9 78.7 %collective-permute-start.4 = (f32[8,96,384]{2,0,1:T(8,128)}, f32[8,96,384]{2,0,1:T(8,128)}, u32[]{:S(2)}, u32[]{:S(2)}) collective-permute-start(f32[8,96,384]{2,0,1:T(8,128)} %get-tuple-element.31), channel_id=1, source_target_pairs={{0,16},{8,24},{16,0},{24,8},{1,17},{9,25},{17,1},{25,9},{2,18},{10... | collective-permute-start | bytes 3538952 | tf_op jit(solution)/shard_map/ppermute | solution.py:407
  312.7 80.3 %collective-permute-start.3 = (f32[8,96,384]{2,0,1:T(8,128)}, f32[8,96,384]{2,0,1:T(8,128)}, u32[]{:S(2)}, u32[]{:S(2)}) collective-permute-start(f32[8,96,384]{2,0,1:T(8,128)} %get-tuple-element.29), channel_id=1, source_target_pairs={{0,8},{8,16},{16,24},{24,0},{1,9},{9,17},{17,25},{25,1},{2,10},{10... | collective-permute-start | bytes 3538952 | tf_op jit(solution)/shard_map/ppermute | solution.py:407
  314.1 75.5 %copy-start.11 = (f32[4,96,384]{2,1,0:T(8,128)S(1)}, f32[4,96,384]{2,1,0:T(8,128)}, u32[]{:S(2)}) copy-start(f32[4,96,384]{2,1,0:T(8,128)} %constant.267) | copy-start | bytes 1769476
  317.6 80.9 %slice-start.2 = ((s8[4718592]{0:T(1024)(128)(4,1)}), s8[4194304]{0:T(1024)(128)(4,1)S(1)}, s32[]{:S(2)}) async-start(s8[4718592]{0:T(1024)(128)(4,1)} %bitcast.203), calls=%async_computation.8 | async-start | bytes 8388608
  321.1 77.4 %slice-start.3 = ((s8[4718592]{0:T(1024)(128)(4,1)}), s8[524288]{0:T(1024)(128)(4,1)S(1)}, s32[]{:S(2)}) async-start(s8[4718592]{0:T(1024)(128)(4,1)} %bitcast.203), calls=%async_computation.9 | async-start | bytes 1048576
  321.1 77.4 %copy-start.9 = (f32[8,48,384,1]{2,1,3,0:T(8,128)S(1)}, f32[8,48,384,1]{2,1,3,0:T(8,128)}, u32[]{:S(2)}) copy-start(f32[8,48,384,1]{2,1,3,0:T(8,128)} %constant.272) | copy-start | bytes 1769476
  398.5 11.1 %copy-start.3 = (f32[4,96,384,1,1]{2,1,0,4,3:T(8,128)S(1)}, f32[4,96,384,1,1]{2,1,0,4,3:T(8,128)}, u32[]{:S(2)}) copy-start(f32[4,96,384,1,1]{2,1,0,4,3:T(8,128)} %constant.270) | copy-start | bytes 1769476
  428.3 9.6 %copy-start.12 = (f32[4,96,384]{2,1,0:T(8,128)S(1)}, f32[4,96,384]{2,1,0:T(8,128)}, u32[]{:S(2)}) copy-start(f32[4,96,384]{2,1,0:T(8,128)} %constant.267) | copy-start | bytes 1769476
  429.8 166.9 %all-to-all-start.4 = ((f32[32,288,128]{2,1,0:T(8,128)}), f32[32,288,128]{2,1,0:T(8,128)}, u32[]{:S(2)}, u32[]{:S(2)}) async-start(f32[32,288,128]{2,1,0:T(8,128)} %reshape.173), calls=%async_computation.4 | async-start | bytes 9437184 | tf_op jit(solution)/shard_map/all_to_all | solution.py:323
  433.7 74.6 %collective-permute-start.2 = (f32[8,96,384]{2,0,1:T(8,128)}, f32[8,96,384]{2,0,1:T(8,128)}, u32[]{:S(2)}, u32[]{:S(2)}) collective-permute-start(f32[8,96,384]{2,0,1:T(8,128)} %get-tuple-element.33), channel_id=1, source_target_pairs={{0,24},{8,0},{16,8},{24,16},{1,25},{9,1},{17,9},{25,17},{2,26},{10... | collective-permute-start | bytes 3538952 | tf_op jit(solution)/shard_map/ppermute | solution.py:407
  436.4 75.5 %collective-permute-start.1 = (f32[8,96,384]{2,0,1:T(8,128)}, f32[8,96,384]{2,0,1:T(8,128)S(1)}, u32[]{:S(2)}, u32[]{:S(2)}) collective-permute-start(f32[8,96,384]{2,0,1:T(8,128)} %get-tuple-element.34), channel_id=1, source_target_pairs={{0,16},{8,24},{16,0},{24,8},{1,17},{9,25},{17,1},{25,9},{2,18},{10... | collective-permute-start | bytes 3538952 | tf_op jit(solution)/shard_map/ppermute | solution.py:407
  436.9 105.9 %collective-permute-start = (f32[8,96,384]{2,0,1:T(8,128)}, f32[8,96,384]{2,0,1:T(8,128)S(1)}, u32[]{:S(2)}, u32[]{:S(2)}) collective-permute-start(f32[8,96,384]{2,0,1:T(8,128)} %get-tuple-element.35), channel_id=1, source_target_pairs={{0,8},{8,16},{16,24},{24,0},{1,9},{9,17},{17,25},{25,1},{2,10},{10... | collective-permute-start | bytes 3538952 | tf_op jit(solution)/shard_map/ppermute | solution.py:407
  508.4 38.3 %slice-start.4 = ((s8[7077888]{0:T(1024)(128)(4,1)}), s8[4194304]{0:T(1024)(128)(4,1)S(1)}, s32[]{:S(2)}) async-start(s8[7077888]{0:T(1024)(128)(4,1)} %bitcast.206), calls=%async_computation.10 | async-start | bytes 8388608
  511.9 34.9 %slice-start.5 = ((s8[7077888]{0:T(1024)(128)(4,1)}), s8[2883584]{0:T(1024)(128)(4,1)S(1)}, s32[]{:S(2)}) async-start(s8[7077888]{0:T(1024)(128)(4,1)} %bitcast.206), calls=%async_computation.11 | async-start | bytes 5767168
  596.7 36.6 %all-to-all-start.5 = ((f32[16,288,128]{2,1,0:T(8,128)}), f32[16,288,128]{2,1,0:T(8,128)}, u32[]{:S(2)}, u32[]{:S(2)}) async-start(f32[16,288,128]{2,1,0:T(8,128)} %reshape.172), calls=%async_computation.5 | async-start | bytes 4718592 | tf_op jit(solution)/shard_map/all_to_all | solution.py:323
  (10 other events, 42.9 us)
